TPU v7x, 32 devices: a whole 2x2x4 slice. The times are simulated.
32 devices in a mesh: seq: 16 (over z, x, core), head: 2 (over y).
Axes of the slice: x: 2, y: 2, z: 4, core: 2. Of those that a mesh axis runs over, the one named last changes fastest.
Arguments:
- query_rows: bfloat16 [8192, 64, 128], P('seq', 'head'), may hold values from -6 to 6
- key_rows: bfloat16 [8192, 64, 128], P('seq', 'head'), may hold values from -6 to 6
- value_rows: bfloat16 [8192, 64, 128], P('seq', 'head'), may hold values from -6 to 6
- log_decay: float32 [8192, 64], P('seq', 'head'), may hold values from -1.5 to 0, as said below
- state_in: float32 [128, 64, 128], P(None, 'head'), may hold values from -768 to 768
- decode_query: bfloat16 [8, 64, 128], P(None, 'head'), may hold values from -6 to 6
- decode_key: bfloat16 [8, 64, 128], P(None, 'head'), may hold values from -6 to 6
- decode_value: bfloat16 [8, 64, 128], P(None, 'head'), may hold values from -6 to 6
- decode_decay: float32 [8, 64], P(None, 'head'), may hold values from -0.5 to -0.02
Outputs:
- attended: bfloat16 [8192, 64, 128], P('seq', 'head')
- final_state: float32 [128, 64, 128], P('seq', 'head')
- decode_out: float32 [8, 64, 128], P(None, 'head')
Inputs may be any that keep to these rules, and one draw needn't show every extreme that they name: log_decay is never positive.
All inputs are finite; a program needn't handle non-finite values.
Results may differ from a plain program's by a relative error of at most 0.0035.
Values sent between devices are 32-bit elements; how exact they have to be, the bound alone decides.
No kernel may reach another device: no remote copies, remote signals or barrier semaphores. Data moves between devices by JAX's collectives and lax.ppermute only.
A program may use at most 64 MiB of HBM per device.

v0:
```python
import functools

import jax
import jax.numpy as jnp
from jax import lax
from jax.experimental import pallas as pl
from jax.experimental.pallas import tpu as pltpu
from jax.sharding import PartitionSpec as P

norm_eps = 1e-06
LANES = 128
SUB = 8
HIGH = lax.Precision.HIGHEST
F32 = jnp.float32
BF16 = jnp.bfloat16


def split3(x):
    hi = x.astype(BF16)
    rest = x - hi.astype(F32)
    mid = rest.astype(BF16)
    low = (rest - mid.astype(F32)).astype(BF16)
    return hi, mid, low


def split2(x):
    hi = x.astype(BF16)
    return hi, (x - hi.astype(F32)).astype(BF16)


def triangle_sum(rows, keep):
    tokens = rows.shape[1]
    s = lax.broadcasted_iota(jnp.int32, (tokens, tokens), 0)
    t = lax.broadcasted_iota(jnp.int32, (tokens, tokens), 1)
    ones = jnp.where(keep(s, t), 1.0, 0.0).astype(BF16)
    total = None
    for piece in split3(rows):
        part = jnp.dot(piece, ones, preferred_element_type=F32)
        total = part if total is None else total + part
    return total


def columns_of(rows):
    return jnp.transpose(rows, (1, 0))


def by_head(ref, scratch):
    tokens, heads, width = ref.shape
    scratch[...] = ref[...].astype(F32).reshape(tokens * heads, width)


def head_rows(scratch, head):
    return scratch[pl.ds(head, scratch.shape[0] // SUB, stride=SUB), :]


def state_kernel(tiled, pseudo, rows, ld_ref, k_ref, v_ref, qd_ref, pos_ref, *refs):
    if tiled:
        keep_ref, send_ref, tot_ref, kf, vf = refs
    else:
        state_ref, tot_ref, kf, vf = refs
    group = pl.program_id(0)
    decays = ld_ref[...]
    tot_ref[...] = jnp.broadcast_to(jnp.sum(decays, axis=1, keepdims=True), (SUB, LANES))
    to_end = columns_of(jnp.exp(triangle_sum(decays, lambda s, t: s > t)))
    by_head(k_ref, kf)
    by_head(v_ref, vf)
    if tiled:
        core, xbit = pos_ref[0] == 1, pos_ref[1] == 1

    def place(slot, square):
        spans = square.shape[0] // (4 * rows)
        for z in range(spans):
            piece = [square[(z * 4 + i) * rows : (z * 4 + i + 1) * rows] for i in range(4)]
            for x_rel in range(2):
                def pick(c_rel):
                    near = jnp.where(core, piece[2 * x_rel + 1 - c_rel], piece[2 * x_rel + c_rel])
                    far = jnp.where(core, piece[2 * (1 - x_rel) + 1 - c_rel], piece[2 * (1 - x_rel) + c_rel])
                    return jnp.where(xbit, far, near)
                keep_ref[x_rel, z, slot] = pick(0)
                send_ref[x_rel, z, slot] = pick(1)

    readings = []
    for i in range(SUB):
        keys = head_rows(kf, i).astype(BF16)
        weighted = head_rows(vf, i) * to_end[:, i : i + 1]
        hi, low = split2(weighted)
        both = lax.dot_general(keys, jnp.concatenate([hi, low], axis=1), (((0,), (0,)), ((), ())), preferred_element_type=F32)
        state = both[:, :LANES] + both[:, LANES:]
        if pseudo:
            hi, low = split2(state)
            read = jnp.dot(qd_ref[i], jnp.concatenate([hi, low], axis=1), preferred_element_type=F32)
            readings.append(read[:, :LANES] + read[:, LANES:])
        if tiled:
            place(group * SUB + i, state)
        else:
            state_ref[i] = state
    if pseudo:
        slot = keep_ref.shape[2] - 1
        half = SUB // 4
        for zz in range(half):
            piece = readings[4 * zz : 4 * zz + 4]
            for x_rel in range(2):
                def pick(c_rel):
                    near = jnp.where(core, piece[2 * x_rel + 1 - c_rel], piece[2 * x_rel + c_rel])
                    far = jnp.where(core, piece[2 * (1 - x_rel) + 1 - c_rel], piece[2 * (1 - x_rel) + c_rel])
                    return jnp.where(xbit, far, near)
                keep_ref[x_rel, group * half + zz, slot] = pick(0)
                send_ref[x_rel, group * half + zz, slot] = pick(1)


def states(chunk, heads, tiled, pseudo, rows, spans, pos, decays, key_rows, value_rows, dec_query):
    tokens, _, width = key_rows.shape
    groups = heads // SUB
    first = chunk * groups
    slots = heads + (1 if pseudo else 0)
    block = pl.BlockSpec((tokens, SUB, width), lambda g: (0, first + g, 0))
    tot = jax.ShapeDtypeStruct((heads, LANES), F32)
    tot_spec = pl.BlockSpec((SUB, LANES), lambda g: (g, 0))
    if tiled:
        shape = jax.ShapeDtypeStruct((2, spans, slots, rows, width), F32)
        whole = pl.BlockSpec((2, spans, slots, rows, width), lambda g: (0, 0, 0, 0, 0))
        out_shape, out_specs = (shape, shape, tot), (whole, whole, tot_spec)
    else:
        out_shape = (jax.ShapeDtypeStruct((heads, width, width), F32), tot)
        out_specs = (pl.BlockSpec((SUB, width, width), lambda g: (g, 0, 0)), tot_spec)
    return pl.pallas_call(
        functools.partial(state_kernel, tiled, pseudo, rows),
        grid=(groups,),
        in_specs=[
            pl.BlockSpec((SUB, tokens), lambda g: (first + g, 0)),
            block,
            block,
            pl.BlockSpec((SUB,) + dec_query.shape[1:], lambda g: (first + g, 0, 0)),
            pl.BlockSpec(memory_space=pltpu.SMEM),
        ],
        out_specs=out_specs,
        out_shape=out_shape,
        scratch_shapes=[pltpu.VMEM((tokens * SUB, width), F32)] * 2,
        cost_estimate=pl.CostEstimate(flops=4 * heads * tokens * width * width, transcendentals=heads * tokens, bytes_accessed=4 * heads * tokens * width),
        name="states",
    )(decays, key_rows, value_rows, dec_query, pos)


def intra_kernel(tile, ld_ref, q_ref, k_ref, v_ref, intra_ref, qh_ref, qf, kf, vf):
    tokens = q_ref.shape[0]
    cum = triangle_sum(ld_ref[...], lambda s, t: s <= t)
    cols = columns_of(cum)
    by_head(q_ref, qf)
    by_head(k_ref, kf)
    by_head(v_ref, vf)
    row = lax.broadcasted_iota(jnp.int32, (tile, tile), 0)
    col = lax.broadcasted_iota(jnp.int32, (tile, tile), 1)
    causal = row >= col
    for i in range(SUB):
        queries = head_rows(qf, i).astype(BF16)
        keys = head_rows(kf, i).astype(BF16)
        values = head_rows(vf, i).astype(BF16)
        qh_ref[i] = queries
        for start in range(0, tokens, tile):
            end = start + tile
            scores = lax.dot_general(queries[start:end], keys[:end], (((1,), (1,)), ((), ())), preferred_element_type=F32)
            gaps = cols[start:end, i : i + 1] - cum[i : i + 1, :end]
            inside = jnp.where(causal, gaps[:, start:], -jnp.inf)
            if start:
                gaps = jnp.concatenate([gaps[:, :start], inside], axis=1)
            else:
                gaps = inside
            masked = (scores * jnp.exp(gaps)).astype(BF16)
            intra_ref[i, start:end] = jnp.dot(masked, values[:end], preferred_element_type=F32)


def inside_blocks(group, count, decays, query_rows, key_rows, value_rows):
    tokens, _, width = query_rows.shape
    block = pl.BlockSpec((tokens, SUB, width), lambda g: (0, group + g, 0))
    out = pl.BlockSpec((SUB, tokens, width), lambda g: (g, 0, 0))
    return pl.pallas_call(
        functools.partial(intra_kernel, 128),
        grid=(count,),
        in_specs=[pl.BlockSpec((SUB, tokens), lambda g: (group + g, 0)), block, block, block],
        out_specs=(out, out),
        out_shape=(
            jax.ShapeDtypeStruct((count * SUB, tokens, width), F32),
            jax.ShapeDtypeStruct((count * SUB, tokens, width), BF16),
        ),
        scratch_shapes=[pltpu.VMEM((tokens * SUB, width), F32)] * 3,
        cost_estimate=pl.CostEstimate(flops=4 * count * SUB * tokens * tokens * width, transcendentals=count * SUB * tokens * tokens, bytes_accessed=12 * count * SUB * tokens * width),
        name="inside",
    )(decays, query_rows, key_rows, value_rows)


def output_kernel(tiled, ld_ref, qh_ref, intra_ref, *refs):
    if tiled:
        near_ref, far_ref, pos_ref, out_ref, flat = refs
        core, xbit = pos_ref[0] == 1, pos_ref[1] == 1
    else:
        state_ref, out_ref, flat = refs
    tokens = out_ref.shape[0]
    cols = columns_of(jnp.exp(triangle_sum(ld_ref[...], lambda s, t: s <= t)))
    for i in range(SUB):
        if tiled:
            pieces = []
            for z in range(near_ref.shape[1]):
                for x in range(2):
                    for c in range(2):
                        first = near_ref if c == 0 else far_ref
                        second = far_ref if c == 0 else near_ref
                        plain = jnp.where(core, second[x, z, i], first[x, z, i])
                        flipped = jnp.where(core, second[1 - x, z, i], first[1 - x, z, i])
                        pieces.append(jnp.where(xbit, flipped, plain))
            carried = jnp.concatenate(pieces, axis=0)
        else:
            carried = state_ref[i]
        hi, low = split2(carried)
        both = jnp.dot(qh_ref[i], jnp.concatenate([hi, low], axis=1), preferred_element_type=F32)
        mixed = intra_ref[i] + cols[:, i : i + 1] * (both[:, :LANES] + both[:, LANES:])
        mean = jnp.mean(mixed * mixed, axis=1, keepdims=True)
        flat[pl.ds(i, tokens, stride=SUB), :] = mixed * lax.rsqrt(mean + norm_eps)
    out_ref[...] = flat[...].reshape(out_ref.shape).astype(BF16)


def outputs(tiled, heads, chunk, decays, qh, intra, pos, *carried):
    tokens, width = qh.shape[1:]
    groups = heads // SUB
    first = chunk * groups
    block = pl.BlockSpec((SUB, tokens, width), lambda g: (g, 0, 0))
    if tiled:
        _, spans, _, rows, _ = carried[0].shape
        part = pl.BlockSpec((2, spans, SUB, rows, width), lambda g: (0, 0, g, 0, 0))
        specs = [part, part, pl.BlockSpec(memory_space=pltpu.SMEM)]
        extra = carried + (pos,)
    else:
        specs = [pl.BlockSpec((SUB, width, width), lambda g: (g, 0, 0))]
        extra = carried
    return pl.pallas_call(
        functools.partial(output_kernel, tiled),
        grid=(groups,),
        in_specs=[pl.BlockSpec((SUB, tokens), lambda g: (first + g, 0)), block, block] + specs,
        out_specs=pl.BlockSpec((tokens, SUB, width), lambda g: (0, g, 0)),
        out_shape=jax.ShapeDtypeStruct((tokens, heads, width), BF16),
        scratch_shapes=[pltpu.VMEM((tokens * SUB, width), F32)],
        cost_estimate=pl.CostEstimate(flops=4 * heads * tokens * width * width, transcendentals=2 * heads * tokens, bytes_accessed=8 * heads * tokens * width),
        name="outputs",
    )(decays, qh, intra, *extra)


def decode_matrix(decay):
    steps = decay.shape[0]
    cum = jnp.cumsum(decay, axis=0)
    order = jnp.arange(steps)
    causal = (order[:, None] >= order[None, :]).reshape((steps, steps) + (1,) * (decay.ndim - 1))
    return jnp.exp(jnp.where(causal, cum[:, None] - cum[None, :], -jnp.inf)), jnp.exp(cum)


def normalize(mixed):
    return mixed * lax.rsqrt(jnp.mean(mixed * mixed, axis=-1, keepdims=True) + norm_eps)


def local(query_rows, key_rows, value_rows, log_decay, state_in, decode_query, decode_key, decode_value, decode_decay):
    tokens, heads, width = query_rows.shape
    steps = decode_query.shape[0]
    n = lax.axis_size("seq")
    me = lax.axis_index("seq")
    spans = n // 4
    rows = width // n
    core, xbit, z = me % 2, (me // 2) % 2, me // 4
    tiled = rows % SUB == 0
    pseudo = tiled and rows == steps and heads % n == 0 and n % SUB == 0 and n * steps == width
    chunks = heads // n if pseudo else 1
    per = heads // chunks
    slots = per + (1 if pseudo else 0)
    pos = jnp.stack([core, xbit]).astype(jnp.int32)
    decays = jnp.transpose(log_decay)
    dec_query = jnp.transpose(decode_query, (1, 0, 2))

    swap_core = [(i, i ^ 1) for i in range(n)]
    swap_x = [(i, i ^ 2) for i in range(n)]
    shift = lambda s: [(i, (i + 4 * s) % n) for i in range(n)]

    def first(flag, a, b):
        return jnp.where(flag == 0, a, b)

    def weights(total, part):
        w = jnp.exp(total)[:, None, :]
        if pseudo:
            lead = part.shape[:-1]
            w = jnp.broadcast_to(w, lead + w.shape)
            w = jnp.concatenate([w, jnp.exp(part)[..., None, None, :]], axis=len(lead))
        return w

    def owners(total, x_rel):
        if not pseudo:
            return None
        t = total.reshape(spans, 2, 2, LANES)
        t = lax.dynamic_index_in_dim(t, core, 2, keepdims=False)
        return lax.dynamic_index_in_dim(t, (xbit + x_rel) % 2, 1, keepdims=False)

    def exchange(x, total, pairs):
        flat = jnp.concatenate([x.reshape(-1, width), total], axis=0)
        got = lax.ppermute(flat, "seq", pairs)
        return got[: -total.shape[0]].reshape(x.shape), got[-total.shape[0] :]

    def to_absolute(pieces):
        turned = jnp.stack(pieces[::-1] + pieces[:0:-1])
        return lax.dynamic_slice_in_dim(turned, spans - 1 - z, spans, 0)

    if pseudo:
        def own_head(x, axis, c):
            return lax.dynamic_index_in_dim(x, c * n + me, axis, keepdims=False)

        dec_terms = []
        for c in range(chunks):
            q, k, v, d = (own_head(a, 1, c).astype(F32) for a in (decode_query, decode_key, decode_value, decode_decay))
            pair, from_end = decode_matrix(d)
            near = jnp.dot(jnp.dot(q, k.T, precision=HIGH) * pair, v, precision=HIGH)
            before = jnp.dot(q, own_head(state_in, 1, c), precision=HIGH)
            dec_terms.append((from_end[:, None], near, before))
    prior = jnp.transpose(lax.dynamic_slice_in_dim(state_in, me * rows, rows, 0), (1, 0, 2))

    kept = []
    for c in range(chunks):
        made = states(c, per, tiled, pseudo, rows, spans, pos, decays, key_rows, value_rows, dec_query)
        if tiled:
            keep, send, total = made
        else:
            whole, total = made
            parts = jnp.transpose(whole.reshape(per, spans, 2, 2, rows, width), (3, 2, 1, 0, 4, 5))
            parts = jnp.where(xbit == 0, parts, parts[:, ::-1])
            keep, send = first(core, parts[0], parts[1]), first(core, parts[1], parts[0])
        kept.append((keep, send, total))

    groups = heads // SUB
    insides = [inside_blocks(c * (groups // chunks), groups // chunks, decays, query_rows, key_rows, value_rows) for c in range(chunks)]

    level = []
    for c in range(chunks):
        keep, send, total = kept[c]
        got, got_total = exchange(send, total, swap_core)
        part = lambda t: jnp.stack([owners(t, 0), owners(t, 1)]) if pseudo else None
        mine = first(core, weights(got_total, part(got_total)), 1.0)
        theirs = first(core, 1.0, weights(total, part(total)))
        chip = keep * mine + got * theirs
        chip_total = total + got_total
        got_x, got_x_total = exchange(chip[1], chip_total, swap_x)
        mine = first(xbit, weights(got_x_total, owners(got_x_total, 0)), 1.0)
        theirs = first(xbit, 1.0, weights(chip_total, owners(chip_total, 0)))
        span = chip[0] * mine + got_x * theirs
        level.append((got, got_total, chip, chip_total, got_x, got_x_total, span, chip_total + got_x_total))

    finals, decoded, carries = [], [], []
    for c in range(chunks):
        span, span_total = level[c][6:]
        pieces = [lax.dynamic_index_in_dim(span, z, 0, keepdims=False)]
        totals = [span_total]
        for s in range(1, spans):
            piece, t = exchange(lax.dynamic_index_in_dim(span, (z + s) % spans, 0, keepdims=False), span_total, shift(s))
            pieces.append(piece)
            totals.append(t)
        pieces, totals = to_absolute(pieces), to_absolute(totals)
        carried = prior[c * per : (c + 1) * per]
        if pseudo:
            carried = jnp.concatenate([carried, dec_terms[c][2][None]], axis=0)
        all_carried = []
        for s in range(spans):
            all_carried.append(carried)
            t = totals[s]
            own = lax.dynamic_index_in_dim(t, me, 0, keepdims=False) if pseudo else None
            carried = carried * weights(t, own) + pieces[s]
        finals.append(carried[:per])
        if pseudo:
            from_end, near, _ = dec_terms[c]
            dec = normalize(carried[per] * from_end + near)
            all_carried = [jnp.concatenate([a[:per], dec[None]], axis=0) for a in all_carried]
        all_carried = jnp.stack(all_carried)
        pieces = [lax.dynamic_index_in_dim(all_carried, z, 0, keepdims=False)]
        for s in range(1, spans):
            pieces.append(lax.ppermute(lax.dynamic_index_in_dim(all_carried, (z + s) % spans, 0, keepdims=False), "seq", shift(s)))
        carries.append(to_absolute(pieces))

    def advance(carried, total, state):
        new = carried[..., :per, :, :] * jnp.exp(total)[:, None, :] + state[..., :per, :, :]
        return jnp.concatenate([new, carried[..., per:, :, :]], axis=-3) if pseudo else new

    attended, dec_out = [], []
    for c in range(chunks):
        keep, send, total = kept[c]
        got, got_total, chip, chip_total, got_x, got_x_total, _, _ = level[c]
        at_span = carries[c]
        msg = first(xbit, advance(at_span, chip_total, chip[0]), at_span)
        own = first(xbit, at_span, advance(at_span, got_x_total, got_x))
        at_chip = jnp.stack([own, lax.ppermute(msg, "seq", swap_x)])
        msg = first(core, advance(at_chip, total, keep), at_chip)
        own = first(core, at_chip, advance(at_chip, got_total, got))
        other = lax.ppermute(msg, "seq", swap_core)
        intra, qh = insides[c]
        if tiled:
            carried = (own, other)
        else:
            both = jnp.stack([first(core, own, other), first(core, other, own)])
            both = jnp.where(xbit == 0, both, both[:, ::-1])
            carried = (jnp.transpose(both, (3, 2, 1, 0, 4, 5)).reshape(per, width, width),)
        attended.append(outputs(tiled, per, c, decays, qh, intra, pos, *carried))
        if pseudo:
            both = jnp.stack([first(core, own[:, :, per], other[:, :, per]), first(core, other[:, :, per], own[:, :, per])])
            both = jnp.where(xbit == 0, both, both[:, ::-1])
            dec_out.append(jnp.transpose(both, (3, 2, 1, 0, 4)).reshape(steps, per, width))

    attended = jnp.concatenate(attended, axis=1)
    final_rows = jnp.transpose(jnp.concatenate(finals, axis=0), (1, 0, 2))
    if pseudo:
        decode_out = jnp.concatenate(dec_out, axis=1)
    else:
        start = me * rows
        key_part = lax.dynamic_slice_in_dim(decode_key, start, rows, 2).astype(F32)
        query_part = lax.dynamic_slice_in_dim(decode_query, start, rows, 2).astype(F32)
        pair, from_end = decode_matrix(decode_decay)
        scores = jnp.einsum("thr,shr->tsh", query_part, key_part, precision=HIGH) * pair
        near = jnp.einsum("tsh,she->the", scores, decode_value.astype(F32), precision=HIGH)
        far = jnp.einsum("thr,rhe->the", query_part, final_rows, precision=HIGH) * from_end[:, :, None]
        decode_out = normalize(lax.psum(near + far, "seq"))
    return attended, final_rows, decode_out


def solution(mesh):
    in_specs = (
        P("seq", "head", None),
        P("seq", "head", None),
        P("seq", "head", None),
        P("seq", "head"),
        P(None, "head", None),
        P(None, "head", None),
        P(None, "head", None),
        P(None, "head", None),
        P(None, "head"),
    )
    out_specs = (P("seq", "head", None), P("seq", "head", None), P(None, "head", None))
    return jax.shard_map(local, mesh=mesh, in_specs=in_specs, out_specs=out_specs, check_vma=False)
```

profile of v0, /device:TPU:0, one launch (start us, length us, event | category | flops | bytes accessed | tf_op | source)
XLA Modules:
  0.0 134.4 jit_solution(361613019093410141)
XLA Ops:
  2.8 6.8 %states.2 = (f32[2,4,17,8,128]{4,3,2,1,0:T(8,128)}, f32[2,4,17,8,128]{4,3,2,1,0:T(8,128)}, f32[16,128]{1,0:T(8,128)}) custom-call(f32[32,512]{1,0:T(8,128)} %bitcast.379, bf16[512,32,128]{2,1,0:T(8,128)(2,1)} %k_ref.7, bf16[512,32,128]{2,1,0:T(8,128)(2,1)} %v_ref.7, bf16[32,8,128]{2,1,0:T(8,128)(2,1)} %bitcast.388, s32[2]{0:T(128)} %pad_add_fusion.pos_ref.refs_2_), custom_call_target="tpu_custom_call" | custom-call | flops 536870912 | bytes 4194304 | tf_op jit(solution)/shard_map/states/pallas_call | solution.py:126
  11.3 6.8 %states.3 = (f32[2,4,17,8,128]{4,3,2,1,0:T(8,128)}, f32[2,4,17,8,128]{4,3,2,1,0:T(8,128)}, f32[16,128]{1,0:T(8,128)}) custom-call(f32[32,512]{1,0:T(8,128)} %bitcast.380, bf16[512,32,128]{2,1,0:T(8,128)(2,1)} %k_ref.7, bf16[512,32,128]{2,1,0:T(8,128)(2,1)} %v_ref.7, bf16[32,8,128]{2,1,0:T(8,128)(2,1)} %bitcast.389, s32[2]{0:T(128)} %pad_add_fusion.pos_ref.refs_2_), custom_call_target="tpu_custom_call" | custom-call | flops 536870912 | bytes 4194304 | tf_op jit(solution)/shard_map/states/pallas_call | solution.py:126
  19.4 12.6 %inside.3 = (f32[16,512,128]{2,1,0:T(8,128)}, bf16[16,512,128]{2,1,0:T(8,128)(2,1)}) custom-call(f32[32,512]{1,0:T(8,128)} %bitcast.381, bf16[512,32,128]{2,1,0:T(8,128)(2,1)} %q_ref.3, bf16[512,32,128]{2,1,0:T(8,128)(2,1)} %k_ref.7, bf16[512,32,128]{2,1,0:T(8,128)(2,1)} %v_ref.7), custom_call_target="tpu_custom_call" | custom-call | flops 2147483648 | bytes 12582912 | tf_op jit(solution)/shard_map/inside/pallas_call | solution.py:176
  32.1 12.9 %inside.2 = (f32[16,512,128]{2,1,0:T(8,128)}, bf16[16,512,128]{2,1,0:T(8,128)(2,1)}) custom-call(f32[32,512]{1,0:T(8,128)} %bitcast.382, bf16[512,32,128]{2,1,0:T(8,128)(2,1)} %q_ref.3, bf16[512,32,128]{2,1,0:T(8,128)(2,1)} %k_ref.7, bf16[512,32,128]{2,1,0:T(8,128)(2,1)} %v_ref.7), custom_call_target="tpu_custom_call" | custom-call | flops 2147483648 | bytes 12582912 | tf_op jit(solution)/shard_map/inside/pallas_call | solution.py:176
  49.9 1.9 %constant_dynamic-slice_fusion.38 = (f32[128,1,128]{2,1,0:T(1,128)}, f32[128,1,128]{2,1,0:T(1,128)}) fusion(f32[128,32,128]{2,1,0:T(8,128)} %param.13, s32[]{:T(128)S(6)} %select_n.387, s32[]{:T(128)S(6)} %select_n.417), kind=kLoop, calls=%fused_computation.216 | loop fusion | bytes 262152 | tf_op jit(solution)/shard_map/jit(dynamic_index_in_dim)/dynamic_slice | solution.py:308
  56.2 2.9 %collective-permute-start.1 = (f32[560,128]{1,0:T(8,128)S(1)}, f32[560,128]{1,0:T(8,128)S(1)}, u32[]{:S(2)}, u32[]{:S(2)}) collective-permute-start(f32[560,128]{1,0:T(8,128)S(1)} %pad_maximum_fusion.13), channel_id=1, source_target_pairs={{0,4},{2,6},{4,0},{6,2},{8,12},{10,14},{12,8},{14,10},{16,20},{18,... | collective-permute-start | bytes 860168 | tf_op jit(solution)/shard_map/ppermute | solution.py:299
  59.8 7.0 %collective-permute-done.1 = f32[560,128]{1,0:T(8,128)S(1)} collective-permute-done((f32[560,128]{1,0:T(8,128)S(1)}, f32[560,128]{1,0:T(8,128)S(1)}, u32[]{:S(2)}, u32[]{:S(2)}) %collective-permute-start.1) | collective-permute-done | bytes 286752 | tf_op jit(solution)/shard_map/ppermute | solution.py:299
  67.0 2.1 %collective-permute-start.4 = (f32[152,128]{1,0:T(8,128)S(1)}, f32[152,128]{1,0:T(8,128)S(1)}, u32[]{:S(2)}, u32[]{:S(2)}) collective-permute-start(f32[152,128]{1,0:T(8,128)S(1)} %get-tuple-element.118), channel_id=1, source_target_pairs={{0,8},{2,10},{4,12},{6,14},{8,16},{10,18},{12,20},{14,22},{16,24},... | collective-permute-start | bytes 233480 | tf_op jit(solution)/shard_map/ppermute | solution.py:299
  69.2 2.6 %collective-permute-start.3 = (f32[152,128]{1,0:T(8,128)S(1)}, f32[152,128]{1,0:T(8,128)S(1)}, u32[]{:S(2)}, u32[]{:S(2)}) collective-permute-start(f32[152,128]{1,0:T(8,128)S(1)} %get-tuple-element.119), channel_id=1, source_target_pairs={{0,16},{2,18},{4,20},{6,22},{8,24},{10,26},{12,28},{14,30},{16,0},... | collective-permute-start | bytes 233480 | tf_op jit(solution)/shard_map/ppermute | solution.py:299
  74.6 2.6 %collective-permute-start.13 = (f32[152,128]{1,0:T(8,128)S(1)}, f32[152,128]{1,0:T(8,128)S(1)}, u32[]{:S(2)}, u32[]{:S(2)}) collective-permute-start(f32[152,128]{1,0:T(8,128)S(1)} %get-tuple-element.126), channel_id=1, source_target_pairs={{0,16},{2,18},{4,20},{6,22},{8,24},{10,26},{12,28},{14,30},{16,0},... | collective-permute-start | bytes 233480 | tf_op jit(solution)/shard_map/ppermute | solution.py:299
  77.1 2.9 %collective-permute-start.12 = (f32[152,128]{1,0:T(8,128)S(1)}, f32[152,128]{1,0:T(8,128)S(1)}, u32[]{:S(2)}, u32[]{:S(2)}) collective-permute-start(f32[152,128]{1,0:T(8,128)S(1)} %get-tuple-element.127), channel_id=1, source_target_pairs={{0,24},{2,26},{4,28},{6,30},{8,0},{10,2},{12,4},{14,6},{16,8},{18,... | collective-permute-start | bytes 233480 | tf_op jit(solution)/shard_map/ppermute | solution.py:299
  80.1 2.9 %collective-permute-done.12 = f32[152,128]{1,0:T(8,128)S(1)} collective-permute-done((f32[152,128]{1,0:T(8,128)S(1)}, f32[152,128]{1,0:T(8,128)S(1)}, u32[]{:S(2)}, u32[]{:S(2)}) %collective-permute-start.12) | collective-permute-done | bytes 77856 | tf_op jit(solution)/shard_map/ppermute | solution.py:299
  83.9 1.6 %collective-permute-start.7 = (f32[17,8,128]{2,1,0:T(8,128)S(1)}, f32[17,8,128]{2,1,0:T(8,128)S(1)}, u32[]{:S(2)}, u32[]{:S(2)}) collective-permute-start(f32[17,8,128]{2,1,0:T(8,128)S(1)} %get-tuple-element.76), channel_id=1, source_target_pairs={{0,8},{2,10},{4,12},{6,14},{8,16},{10,18},{12,20},{14,22},{16,24},... | collective-permute-start | bytes 208904 | tf_op jit(solution)/shard_map/ppermute | solution.py:376
  85.6 2.2 %collective-permute-start.6 = (f32[17,8,128]{2,1,0:T(8,128)S(1)}, f32[17,8,128]{2,1,0:T(8,128)S(1)}, u32[]{:S(2)}, u32[]{:S(2)}) collective-permute-start(f32[17,8,128]{2,1,0:T(8,128)S(1)} %get-tuple-element.77), channel_id=1, source_target_pairs={{0,16},{2,18},{4,20},{6,22},{8,24},{10,26},{12,28},{14,30},{16,0},... | collective-permute-start | bytes 208904 | tf_op jit(solution)/shard_map/ppermute | solution.py:376
  88.7 1.8 %collective-permute-start.17 = (f32[17,8,128]{2,1,0:T(8,128)S(1)}, f32[17,8,128]{2,1,0:T(8,128)S(1)}, u32[]{:S(2)}, u32[]{:S(2)}) collective-permute-start(f32[17,8,128]{2,1,0:T(8,128)S(1)} %get-tuple-element.86), channel_id=1, source_target_pairs={{0,8},{2,10},{4,12},{6,14},{8,16},{10,18},{12,20},{14,22},{16,24},... | collective-permute-start | bytes 208904 | tf_op jit(solution)/shard_map/ppermute | solution.py:376
  91.3 1.9 %collective-permute-done.5 = f32[17,8,128]{2,1,0:T(8,128)S(1)} collective-permute-done((f32[17,8,128]{2,1,0:T(8,128)S(1)}, f32[17,8,128]{2,1,0:T(8,128)S(1)}, u32[]{:S(2)}, u32[]{:S(2)}) %collective-permute-start.5) | collective-permute-done | bytes 69664 | tf_op jit(solution)/shard_map/ppermute | solution.py:376
  93.2 2.5 %collective-permute-start.15 = (f32[17,8,128]{2,1,0:T(8,128)S(1)}, f32[17,8,128]{2,1,0:T(8,128)S(1)}, u32[]{:S(2)}, u32[]{:S(2)}) collective-permute-start(f32[17,8,128]{2,1,0:T(8,128)S(1)} %get-tuple-element.88), channel_id=1, source_target_pairs={{0,24},{2,26},{4,28},{6,30},{8,0},{10,2},{12,4},{14,6},{16,8},{18,... | collective-permute-start | bytes 208904 | tf_op jit(solution)/shard_map/ppermute | solution.py:376
  96.0 1.6 %collective-permute-start.8 = (f32[4,17,8,128]{3,2,1,0:T(8,128)S(1)}, f32[4,17,8,128]{3,2,1,0:T(8,128)S(1)}, u32[]{:S(2)}, u32[]{:S(2)}) collective-permute-start(f32[4,17,8,128]{3,2,1,0:T(8,128)S(1)} %get-tuple-element.65), channel_id=1, source_target_pairs={{0,4},{2,6},{4,0},{6,2},{8,12},{10,14},{12,8},{14,10},{16,20},{18,... | collective-permute-start | bytes 835592 | tf_op jit(solution)/shard_map/ppermute | solution.py:390
  97.6 2.3 %collective-permute-done.15 = f32[17,8,128]{2,1,0:T(8,128)S(1)} collective-permute-done((f32[17,8,128]{2,1,0:T(8,128)S(1)}, f32[17,8,128]{2,1,0:T(8,128)S(1)}, u32[]{:S(2)}, u32[]{:S(2)}) %collective-permute-start.15) | collective-permute-done | bytes 69664 | tf_op jit(solution)/shard_map/ppermute | solution.py:376
  101.8 3.7 %collective-permute-done.8 = f32[4,17,8,128]{3,2,1,0:T(8,128)S(1)} collective-permute-done((f32[4,17,8,128]{3,2,1,0:T(8,128)S(1)}, f32[4,17,8,128]{3,2,1,0:T(8,128)S(1)}, u32[]{:S(2)}, u32[]{:S(2)}) %collective-permute-start.8) | collective-permute-done | bytes 278560 | tf_op jit(solution)/shard_map/ppermute | solution.py:390
  109.8 1.9 %collective-permute-done.19.refs_1_ = f32[2,4,17,8,128]{4,3,2,1,0:T(8,128)S(1)} collective-permute-done((f32[2,4,17,8,128]{4,3,2,1,0:T(8,128)S(1)}, f32[2,4,17,8,128]{4,3,2,1,0:T(8,128)S(1)}, u32[]{:S(2)}, u32[]{:S(2)}) %collective-permute-start.19) | collective-permute-done | bytes 557088 | tf_op jit(solution)/shard_map/ppermute | solution.py:393
  113.5 8.2 %outputs.2 = bf16[512,16,128]{2,1,0:T(8,128)(2,1)} custom-call(f32[32,512]{1,0:T(8,128)} %bitcast.383, bf16[16,512,128]{2,1,0:T(8,128)(2,1)} %get-tuple-element.13.qh_ref, f32[16,512,128]{2,1,0:T(8,128)} %get-tuple-element.14.intra_ref, f32[2,4,17,8,128]{4,3,2,1,0:T(8,128)} %copy.111.refs_0_, f32[2,4,17,8,128]{4,3,2,1,0:T(8,128)} %copy.112.refs_1_, ...), custom_call_target="tpu_custom_call" | custom-call | flops 536870912 | bytes 8388608 | tf_op jit(solution)/shard_map/outputs/pallas_call | solution.py:234
  121.6 8.4 %outputs.3 = bf16[512,16,128]{2,1,0:T(8,128)(2,1)} custom-call(f32[32,512]{1,0:T(8,128)} %bitcast.384, bf16[16,512,128]{2,1,0:T(8,128)(2,1)} %get-tuple-element.18.qh_ref, f32[16,512,128]{2,1,0:T(8,128)} %get-tuple-element.19.intra_ref, f32[2,4,17,8,128]{4,3,2,1,0:T(8,128)} %copy.141.refs_0_, f32[2,4,17,8,128]{4,3,2,1,0:T(8,128)} %copy-done.3, ...), custom_call_target="tpu_custom_call" | custom-call | flops 536870912 | bytes 8388608 | tf_op jit(solution)/shard_map/outputs/pallas_call | solution.py:234
  130.1 4.3 %pad_maximum_fusion = bf16[512,32,128]{2,1,0:T(8,128)(2,1)} fusion(bf16[512,16,128]{2,1,0:T(8,128)(2,1)} %outputs.3, bf16[512,16,128]{2,1,0:T(8,128)(2,1)S(1)} %copy-done), kind=kLoop, calls=%fused_computation | loop fusion | flops 8388608 | bytes 8388608 | tf_op jit(solution)/shard_map/concatenate | solution.py:407
  (230 shorter events, 27.7 us)
Async XLA Ops:
  10.7 45.1 %collective-permute-start = (f32[1104,128]{1,0:T(8,128)S(1)}, f32[1104,128]{1,0:T(8,128)S(1)}, u32[]{:S(2)}, u32[]{:S(2)}) collective-permute-start(f32[1104,128]{1,0:T(8,128)S(1)} %pad_maximum_fusion.6), channel_id=1, source_target_pairs={{0,2},{2,0},{4,6},{6,4},{8,10},{10,8},{12,14},{14,12},{16,18},{18,... | collective-permute-start | bytes 1695752 | tf_op jit(solution)/shard_map/ppermute | solution.py:299
  19.2 39.9 %collective-permute-start.10 = (f32[1104,128]{1,0:T(8,128)S(1)}, f32[1104,128]{1,0:T(8,128)S(1)}, u32[]{:S(2)}, u32[]{:S(2)}) collective-permute-start(f32[1104,128]{1,0:T(8,128)S(1)} %pad_maximum_fusion.7), channel_id=1, source_target_pairs={{0,2},{2,0},{4,6},{6,4},{8,10},{10,8},{12,14},{14,12},{16,18},{18,... | collective-permute-start | bytes 1695752 | tf_op jit(solution)/shard_map/ppermute | solution.py:299
  32.1 22.9 %copy-start.4 = (f32[16,128]{1,0:T(8,128)S(1)}, f32[16,128]{1,0:T(8,128)}, u32[]{:S(2)}) copy-start(f32[16,128]{1,0:T(8,128)} %get-tuple-element.22) | copy-start | bytes 24580
  32.1 23.9 %copy-start.2 = (f32[2,4,17,8,128]{4,3,2,1,0:T(8,128)S(1)}, f32[2,4,17,8,128]{4,3,2,1,0:T(8,128)}, u32[]{:S(2)}) copy-start(f32[2,4,17,8,128]{4,3,2,1,0:T(8,128)} %get-tuple-element.15) | copy-start | bytes 1671172
  56.2 10.6 %collective-permute-start.1 = (f32[560,128]{1,0:T(8,128)S(1)}, f32[560,128]{1,0:T(8,128)S(1)}, u32[]{:S(2)}, u32[]{:S(2)}) collective-permute-start(f32[560,128]{1,0:T(8,128)S(1)} %pad_maximum_fusion.13), channel_id=1, source_target_pairs={{0,4},{2,6},{4,0},{6,2},{8,12},{10,14},{12,8},{14,10},{16,20},{18,... | collective-permute-start | bytes 860168 | tf_op jit(solution)/shard_map/ppermute | solution.py:299
  59.7 23.8 %copy-start.9 = (f32[8]{0:T(128)S(1)}, f32[8]{0:T(128)}, u32[]{:S(2)}) copy-start(f32[8]{0:T(128)} %exp.276) | copy-start | bytes 100
  59.7 23.8 %copy-start.10 = (f32[8,8]{1,0:T(8,128)S(1)}, f32[8,8]{1,0:T(8,128)}, u32[]{:S(2)}) copy-start(f32[8,8]{1,0:T(8,128)} %convolution_multiply_fusion.1) | copy-start | bytes 772
  59.7 13.4 %collective-permute-start.11 = (f32[560,128]{1,0:T(8,128)S(1)}, f32[560,128]{1,0:T(8,128)S(1)}, u32[]{:S(2)}, u32[]{:S(2)}) collective-permute-start(f32[560,128]{1,0:T(8,128)S(1)} %pad_maximum_fusion.14), channel_id=1, source_target_pairs={{0,4},{2,6},{4,0},{6,2},{8,12},{10,14},{12,8},{14,10},{16,20},{18,... | collective-permute-start | bytes 860168 | tf_op jit(solution)/shard_map/ppermute | solution.py:299
  67.0 13.0 %collective-permute-start.4 = (f32[152,128]{1,0:T(8,128)S(1)}, f32[152,128]{1,0:T(8,128)S(1)}, u32[]{:S(2)}, u32[]{:S(2)}) collective-permute-start(f32[152,128]{1,0:T(8,128)S(1)} %get-tuple-element.118), channel_id=1, source_target_pairs={{0,8},{2,10},{4,12},{6,14},{8,16},{10,18},{12,20},{14,22},{16,24},... | collective-permute-start | bytes 233480 | tf_op jit(solution)/shard_map/ppermute | solution.py:299
  69.2 10.9 %collective-permute-start.3 = (f32[152,128]{1,0:T(8,128)S(1)}, f32[152,128]{1,0:T(8,128)S(1)}, u32[]{:S(2)}, u32[]{:S(2)}) collective-permute-start(f32[152,128]{1,0:T(8,128)S(1)} %get-tuple-element.119), channel_id=1, source_target_pairs={{0,16},{2,18},{4,20},{6,22},{8,24},{10,26},{12,28},{14,30},{16,0},... | collective-permute-start | bytes 233480 | tf_op jit(solution)/shard_map/ppermute | solution.py:299
  71.8 5.4 %collective-permute-start.2 = (f32[152,128]{1,0:T(8,128)S(1)}, f32[152,128]{1,0:T(8,128)S(1)}, u32[]{:S(2)}, u32[]{:S(2)}) collective-permute-start(f32[152,128]{1,0:T(8,128)S(1)} %get-tuple-element.120), channel_id=1, source_target_pairs={{0,24},{2,26},{4,28},{6,30},{8,0},{10,2},{12,4},{14,6},{16,8},{18,... | collective-permute-start | bytes 233480 | tf_op jit(solution)/shard_map/ppermute | solution.py:299
  73.4 9.7 %collective-permute-start.14 = (f32[152,128]{1,0:T(8,128)S(1)}, f32[152,128]{1,0:T(8,128)S(1)}, u32[]{:S(2)}, u32[]{:S(2)}) collective-permute-start(f32[152,128]{1,0:T(8,128)S(1)} %get-tuple-element.125), channel_id=1, source_target_pairs={{0,8},{2,10},{4,12},{6,14},{8,16},{10,18},{12,20},{14,22},{16,24},... | collective-permute-start | bytes 233480 | tf_op jit(solution)/shard_map/ppermute | solution.py:299
  74.6 8.5 %collective-permute-start.13 = (f32[152,128]{1,0:T(8,128)S(1)}, f32[152,128]{1,0:T(8,128)S(1)}, u32[]{:S(2)}, u32[]{:S(2)}) collective-permute-start(f32[152,128]{1,0:T(8,128)S(1)} %get-tuple-element.126), channel_id=1, source_target_pairs={{0,16},{2,18},{4,20},{6,22},{8,24},{10,26},{12,28},{14,30},{16,0},... | collective-permute-start | bytes 233480 | tf_op jit(solution)/shard_map/ppermute | solution.py:299
  77.1 5.9 %collective-permute-start.12 = (f32[152,128]{1,0:T(8,128)S(1)}, f32[152,128]{1,0:T(8,128)S(1)}, u32[]{:S(2)}, u32[]{:S(2)}) collective-permute-start(f32[152,128]{1,0:T(8,128)S(1)} %get-tuple-element.127), channel_id=1, source_target_pairs={{0,24},{2,26},{4,28},{6,30},{8,0},{10,2},{12,4},{14,6},{16,8},{18,... | collective-permute-start | bytes 233480 | tf_op jit(solution)/shard_map/ppermute | solution.py:299
  83.9 11.9 %collective-permute-start.7 = (f32[17,8,128]{2,1,0:T(8,128)S(1)}, f32[17,8,128]{2,1,0:T(8,128)S(1)}, u32[]{:S(2)}, u32[]{:S(2)}) collective-permute-start(f32[17,8,128]{2,1,0:T(8,128)S(1)} %get-tuple-element.76), channel_id=1, source_target_pairs={{0,8},{2,10},{4,12},{6,14},{8,16},{10,18},{12,20},{14,22},{16,24},... | collective-permute-start | bytes 208904 | tf_op jit(solution)/shard_map/ppermute | solution.py:376
  85.6 10.2 %collective-permute-start.6 = (f32[17,8,128]{2,1,0:T(8,128)S(1)}, f32[17,8,128]{2,1,0:T(8,128)S(1)}, u32[]{:S(2)}, u32[]{:S(2)}) collective-permute-start(f32[17,8,128]{2,1,0:T(8,128)S(1)} %get-tuple-element.77), channel_id=1, source_target_pairs={{0,16},{2,18},{4,20},{6,22},{8,24},{10,26},{12,28},{14,30},{16,0},... | collective-permute-start | bytes 208904 | tf_op jit(solution)/shard_map/ppermute | solution.py:376
  87.8 5.5 %collective-permute-start.5 = (f32[17,8,128]{2,1,0:T(8,128)S(1)}, f32[17,8,128]{2,1,0:T(8,128)S(1)}, u32[]{:S(2)}, u32[]{:S(2)}) collective-permute-start(f32[17,8,128]{2,1,0:T(8,128)S(1)} %get-tuple-element.78), channel_id=1, source_target_pairs={{0,24},{2,26},{4,28},{6,30},{8,0},{10,2},{12,4},{14,6},{16,8},{18,... | collective-permute-start | bytes 208904 | tf_op jit(solution)/shard_map/ppermute | solution.py:376
  88.7 11.2 %collective-permute-start.17 = (f32[17,8,128]{2,1,0:T(8,128)S(1)}, f32[17,8,128]{2,1,0:T(8,128)S(1)}, u32[]{:S(2)}, u32[]{:S(2)}) collective-permute-start(f32[17,8,128]{2,1,0:T(8,128)S(1)} %get-tuple-element.86), channel_id=1, source_target_pairs={{0,8},{2,10},{4,12},{6,14},{8,16},{10,18},{12,20},{14,22},{16,24},... | collective-permute-start | bytes 208904 | tf_op jit(solution)/shard_map/ppermute | solution.py:376
  90.5 9.4 %collective-permute-start.16 = (f32[17,8,128]{2,1,0:T(8,128)S(1)}, f32[17,8,128]{2,1,0:T(8,128)S(1)}, u32[]{:S(2)}, u32[]{:S(2)}) collective-permute-start(f32[17,8,128]{2,1,0:T(8,128)S(1)} %get-tuple-element.87), channel_id=1, source_target_pairs={{0,16},{2,18},{4,20},{6,22},{8,24},{10,26},{12,28},{14,30},{16,0},... | collective-permute-start | bytes 208904 | tf_op jit(solution)/shard_map/ppermute | solution.py:376
  93.2 6.7 %collective-permute-start.15 = (f32[17,8,128]{2,1,0:T(8,128)S(1)}, f32[17,8,128]{2,1,0:T(8,128)S(1)}, u32[]{:S(2)}, u32[]{:S(2)}) collective-permute-start(f32[17,8,128]{2,1,0:T(8,128)S(1)} %get-tuple-element.88), channel_id=1, source_target_pairs={{0,24},{2,26},{4,28},{6,30},{8,0},{10,2},{12,4},{14,6},{16,8},{18,... | collective-permute-start | bytes 208904 | tf_op jit(solution)/shard_map/ppermute | solution.py:376
  96.0 9.5 %collective-permute-start.8 = (f32[4,17,8,128]{3,2,1,0:T(8,128)S(1)}, f32[4,17,8,128]{3,2,1,0:T(8,128)S(1)}, u32[]{:S(2)}, u32[]{:S(2)}) collective-permute-start(f32[4,17,8,128]{3,2,1,0:T(8,128)S(1)} %get-tuple-element.65), channel_id=1, source_target_pairs={{0,4},{2,6},{4,0},{6,2},{8,12},{10,14},{12,8},{14,10},{16,20},{18,... | collective-permute-start | bytes 835592 | tf_op jit(solution)/shard_map/ppermute | solution.py:390
  100.3 8.3 %collective-permute-start.18 = (f32[4,17,8,128]{3,2,0,1:T(8,128)S(1)}, f32[4,17,8,128]{3,2,0,1:T(8,128)S(1)}, u32[]{:S(2)}, u32[]{:S(2)}) collective-permute-start(f32[4,17,8,128]{3,2,0,1:T(8,128)S(1)} %get-tuple-element.68), channel_id=1, source_target_pairs={{0,4},{2,6},{4,0},{6,2},{8,12},{10,14},{12,8},{14,10},{16,20},{18,... | collective-permute-start | bytes 835592 | tf_op jit(solution)/shard_map/ppermute | solution.py:390
  106.0 3.8 %collective-permute-start.9 = (f32[2,4,17,8,128]{4,3,1,0,2:T(8,128)S(1)}, f32[2,4,17,8,128]{4,3,1,0,2:T(8,128)S(1)}, u32[]{:S(2)}, u32[]{:S(2)}) collective-permute-start(f32[2,4,17,8,128]{4,3,1,0,2:T(8,128)S(1)} %get-tuple-element.48), channel_id=1, source_target_pairs={{0,2},{2,0},{4,6},{6,4},{8,10},{10,8},{12,14},{14,12},{16,18},{18,... | collective-permute-start | bytes 1671176 | tf_op jit(solution)/shard_map/ppermute | solution.py:393
  109.8 2.0 %collective-permute-start.19 = (f32[2,4,17,8,128]{4,3,2,1,0:T(8,128)S(1)}, f32[2,4,17,8,128]{4,3,2,1,0:T(8,128)S(1)}, u32[]{:S(2)}, u32[]{:S(2)}) collective-permute-start(f32[2,4,17,8,128]{4,3,2,1,0:T(8,128)S(1)} %copy.140), channel_id=1, source_target_pairs={{0,2},{2,0},{4,6},{6,4},{8,10},{10,8},{12,14},{14,12},{16,18},{18,... | collective-permute-start | bytes 1671176 | tf_op jit(solution)/shard_map/ppermute | solution.py:393
  (7 other events, 81.2 us)
where the time goes:
time: 135 us; the launch traced here: 134 us
  Pallas kernels  55.8 us (41%)
  starting transfers between devices  28.8 us (21%)
  waiting for transfers between devices  20.7 us (15%)
  local copies, waits for them, and re-layouts  12.8 us (9%)
  other arithmetic  9.57 us (7%)
  matrix products  4.66 us (3%)
  between operations  2.02 us (1%)
    pallas_call x2, Pallas kernels, inside_blocks(): pl.pallas_call(functools.partial(intra_kernel, 128), grid=(count,), in_sp...  25.5 us
    pallas_call x2, Pallas kernels, outputs(): pl.pallas_call(functools.partial(output_kernel, tiled), grid=(groups,), i...  16.6 us
    ppermute x10, starting transfers between devices, exchange(): got = lax.ppermute(flat, 'seq', pairs)  16.4 us
    pallas_call x2, Pallas kernels, states(): pl.pallas_call(functools.partial(state_kernel, tiled, pseudo, rows), grid...  13.6 us
    ppermute x10, waiting for transfers between devices, exchange(): got = lax.ppermute(flat, 'seq', pairs)  9.93 us
    ppermute x6, starting transfers between devices, local(): lax.ppermute(lax.dynamic_index_in_dim(all_carried, (z + s) % spans, 0, ke...  9.2 us
    ppermute x2, waiting for transfers between devices, local(): at_chip = jnp.stack([own, lax.ppermute(msg, 'seq', swap_x)])  4.63 us
    concatenate x1, other arithmetic, local(): attended = jnp.concatenate(attended, axis=1)  4.32 us
  transfers between devices with their start and end apart: 20, of which 7 were waited for; matrix products, arithmetic and copies ran while one was open for 13% of the time, Pallas kernels for 24%

commit v1 on v0

v1 whole, which is shorter than its diff:
```python
import functools

import jax
import jax.numpy as jnp
from jax import lax
from jax.experimental import pallas as pl
from jax.experimental.pallas import tpu as pltpu
from jax.sharding import PartitionSpec as P

norm_eps = 1e-06
LANES = 128
SUB = 8
F32 = jnp.float32
BF16 = jnp.bfloat16
HIGH = lax.Precision.HIGHEST
VM = pl.BlockSpec(memory_space=pltpu.VMEM)
HBM = pl.BlockSpec(memory_space=pltpu.MemorySpace.HBM)
MIB = 1 << 20


def split3(x):
    hi = x.astype(BF16)
    rest = x - hi.astype(F32)
    mid = rest.astype(BF16)
    low = (rest - mid.astype(F32)).astype(BF16)
    return hi, mid, low


def split2(x):
    hi = x.astype(BF16)
    return hi, (x - hi.astype(F32)).astype(BF16)


def exact_dot(x, ones, dims):
    total = None
    for piece in split3(x):
        part = lax.dot_general(piece, ones, (dims, ((), ())), preferred_element_type=F32)
        total = part if total is None else total + part
    return total


def triangle_sum(decays, keep):
    tokens = decays.shape[0]
    s = lax.broadcasted_iota(jnp.int32, (tokens, tokens), 0)
    t = lax.broadcasted_iota(jnp.int32, (tokens, tokens), 1)
    ones = jnp.where(keep(s, t), 1.0, 0.0).astype(BF16)
    return exact_dot(decays, ones, ((0,), (0,)))


def flatten(block, scratch):
    tokens, heads, width = block.shape
    scratch[...] = block.astype(F32).reshape(tokens * heads, width)


def head_rows(scratch, head, heads):
    return scratch[pl.ds(head, scratch.shape[0] // heads, stride=heads), :]


def position():
    me = lax.axis_index("seq")
    return lax.rem(me, 2) == 1, lax.rem(lax.div(me, 2), 2) == 1


def one_group(tiled, pseudo, rows, slot0, group, decay_col, k_block, v_block, dq, head0, kf, vf, outs):
    keep_ref, send_ref, kh_ref, vh_ref = outs
    flatten(k_block, kf)
    flatten(v_block, vf)
    if tiled:
        core, xbit = position()
        spans, slots = keep_ref.shape[1:3]

    def place(slot, z, piece):
        for x_rel in range(2):
            for c_rel in range(2):
                near = jnp.where(core, piece[2 * x_rel + 1 - c_rel], piece[2 * x_rel + c_rel])
                far = jnp.where(core, piece[2 * (1 - x_rel) + 1 - c_rel], piece[2 * (1 - x_rel) + c_rel])
                tile = jnp.where(xbit, far, near)
                if c_rel == 0:
                    keep_ref[x_rel, z, slot] = tile
                else:
                    start = ((x_rel * spans + z) * slots + slot) * rows
                    send_ref[start : start + rows] = tile

    readings = []
    for i in range(SUB):
        keys = head_rows(kf, i, SUB).astype(BF16)
        values = head_rows(vf, i, SUB)
        kh_ref[slot0 + i] = keys
        vh_ref[slot0 + i] = values.astype(BF16)
        hi, low = split2(values * decay_col(i))
        both = lax.dot_general(keys, jnp.concatenate([hi, low], axis=1), (((0,), (0,)), ((), ())), preferred_element_type=F32)
        state = both[:, :LANES] + both[:, LANES:]
        if pseudo:
            hi, low = split2(state)
            query = head_rows(dq, head0 + i, dq.shape[0] // SUB).astype(BF16)
            read = jnp.dot(query, jnp.concatenate([hi, low], axis=1), preferred_element_type=F32)
            readings.append(read[:, :LANES] + read[:, LANES:])
        if tiled:
            for z in range(spans):
                place(slot0 + i, z, [state[(z * 4 + j) * rows : (z * 4 + j + 1) * rows] for j in range(4)])
        else:
            keep_ref[slot0 + i] = state
    for j in range(0, len(readings), 4):
        place(slots - 1, (slot0 + j) // 4, readings[j : j + 4])


def state_kernel(tiled, pseudo, rows, per, lead, *refs):
    tokens = lead[0]
    groups = per // SUB
    first = lead[1] == 0
    heads = lead[2]
    rest = heads - per
    if first:
        refs = list(refs)
        ld_ref, dq_ref, k_hbm, v_hbm = refs[:4]
        keep_ref, send_ref, tot_ref, kh_ref, vh_ref = refs[4:9]
        at = 9
        if rest:
            wcol_ref, tall_ref, krest_ref, vrest_ref = refs[9:13]
            at = 13
        kf, vf, dq, kbuf, vbuf, sems = refs[at:]
        copies = []
        for g in range(groups):
            span = pl.ds(g * SUB, SUB)
            copies.append((
                pltpu.make_async_copy(k_hbm.at[:, span, :], kbuf.at[g], sems.at[2 * g]),
                pltpu.make_async_copy(v_hbm.at[:, span, :], vbuf.at[g], sems.at[2 * g + 1]),
            ))
        if rest:
            span = pl.ds(per, rest)
            copies.append((
                pltpu.make_async_copy(k_hbm.at[:, span, :], krest_ref, sems.at[2 * groups]),
                pltpu.make_async_copy(v_hbm.at[:, span, :], vrest_ref, sems.at[2 * groups + 1]),
            ))
        for pair in copies:
            for copy in pair:
                copy.start()
        decays = ld_ref[...]
        wcol = jnp.transpose(jnp.exp(triangle_sum(decays, lambda s, t: s > t)), (1, 0))
        tall = exact_dot(decays, jnp.ones((tokens, LANES), BF16), ((0,), (0,)))
        totals = tall[:per]
        if rest:
            wcol_ref[...] = wcol
            tall_ref[...] = tall
        head0 = 0
    else:
        wcol_ref, tall_ref, dq_ref, krest_ref, vrest_ref, keep_ref, send_ref, tot_ref, kh_ref, vh_ref, kf, vf, dq = refs
        head0 = lead[1]
        wcol = wcol_ref[...]
        totals = tall_ref[head0 : head0 + per]
    tot_ref[...] = totals
    if tiled:
        send_ref[send_ref.shape[0] - per :] = totals
    if pseudo:
        flatten(dq_ref[...], dq)
    for g in range(groups):
        if first:
            for copy in copies[g]:
                copy.wait()
            k_block, v_block = kbuf[g], vbuf[g]
        else:
            at = head0 - (heads - krest_ref.shape[1]) + g * SUB
            k_block, v_block = krest_ref[:, at : at + SUB, :], vrest_ref[:, at : at + SUB, :]
        base = head0 + g * SUB
        one_group(tiled, pseudo, rows, g * SUB, g, lambda i: wcol[:, base + i : base + i + 1], k_block, v_block, dq, base, kf, vf, (keep_ref, send_ref, kh_ref, vh_ref))
    if first and rest:
        for copy in copies[-1]:
            copy.wait()


def states(chunk, per, tiled, pseudo, rows, spans, arrays):
    first = chunk == 0
    if first:
        log_decay, dec_query, key_rows, value_rows = arrays
        tokens, heads, width = key_rows.shape
    else:
        wcol, tall, dec_query, krest, vrest = arrays
        tokens, heads = wcol.shape
        width = krest.shape[2]
    rest = heads - per
    slots = per + (1 if pseudo else 0)
    if tiled:
        keep = jax.ShapeDtypeStruct((2, spans, slots, rows, width), F32)
        send = jax.ShapeDtypeStruct((2 * spans * slots * rows + per, width), F32)
    else:
        keep = jax.ShapeDtypeStruct((per, width, width), F32)
        send = jax.ShapeDtypeStruct((SUB, width), F32)
    by_head = jax.ShapeDtypeStruct((per, tokens, width), BF16)
    out_shape = [keep, send, jax.ShapeDtypeStruct((per, width), F32), by_head, by_head]
    scratch = [
        pltpu.VMEM((tokens * SUB, width), F32),
        pltpu.VMEM((tokens * SUB, width), F32),
        pltpu.VMEM((dec_query.shape[0] * heads, width), F32),
    ]
    if first:
        if rest:
            out_shape += [jax.ShapeDtypeStruct((tokens, heads), F32), jax.ShapeDtypeStruct((heads, width), F32)]
            out_shape += [jax.ShapeDtypeStruct((tokens, rest, width), BF16)] * 2
        scratch += [pltpu.VMEM((per // SUB, tokens, SUB, width), BF16)] * 2
        scratch += [pltpu.SemaphoreType.DMA((2 * (per // SUB) + 2,))]
        in_specs = [VM, VM, HBM, HBM]
    else:
        in_specs = [VM] * 5
    return pl.pallas_call(
        functools.partial(state_kernel, tiled, pseudo, rows, per, (tokens, chunk * per, heads)),
        in_specs=in_specs,
        out_specs=[VM] * len(out_shape),
        out_shape=out_shape,
        scratch_shapes=scratch,
        cost_estimate=pl.CostEstimate(flops=4 * per * tokens * width * width, transcendentals=per * tokens, bytes_accessed=4 * per * tokens * width),
        compiler_params=pltpu.CompilerParams(vmem_limit_bytes=LIMITS["states"] * MIB),
        name="states",
    )(*arrays)


def inside_kernel(tile, head0, slot0, ld_ref, q_ref, kh_ref, vh_ref, intra_ref, q2_ref, qf):
    tokens = q_ref.shape[0]
    cum = triangle_sum(ld_ref[:, head0 : head0 + SUB], lambda s, t: s <= t)
    cols = jnp.transpose(cum, (1, 0))
    grown = jnp.exp(cols)
    flatten(q_ref[:, head0 : head0 + SUB, :], qf)
    row = lax.broadcasted_iota(jnp.int32, (tile, tile), 0)
    col = lax.broadcasted_iota(jnp.int32, (tile, tile), 1)
    causal = row >= col
    for i in range(SUB):
        wide = head_rows(qf, i, SUB)
        queries = wide.astype(BF16)
        hi, low = split2(wide * grown[:, i : i + 1])
        q2_ref[i, :, :LANES] = hi
        q2_ref[i, :, LANES:] = low
        keys = kh_ref[slot0 + i]
        values = vh_ref[slot0 + i]
        for start in range(0, tokens, tile):
            end = start + tile
            scores = lax.dot_general(queries[start:end], keys[:end], (((1,), (1,)), ((), ())), preferred_element_type=F32)
            gaps = cols[start:end, i : i + 1] - cum[i : i + 1, :end]
            inside = jnp.where(causal, gaps[:, start:], -jnp.inf)
            if start:
                gaps = jnp.concatenate([gaps[:, :start], inside], axis=1)
            else:
                gaps = inside
            masked = (scores * jnp.exp(gaps)).astype(BF16)
            intra_ref[i, start:end] = jnp.dot(masked, values[:end], preferred_element_type=F32)


def inside_block(group, slot0, log_decay, query_rows, kh, vh):
    tokens, _, width = query_rows.shape
    return pl.pallas_call(
        functools.partial(inside_kernel, 128, group * SUB, slot0),
        in_specs=[VM] * 4,
        out_specs=[VM] * 2,
        out_shape=[
            jax.ShapeDtypeStruct((SUB, tokens, width), F32),
            jax.ShapeDtypeStruct((SUB, tokens, 2 * width), BF16),
        ],
        scratch_shapes=[pltpu.VMEM((tokens * SUB, width), F32)],
        cost_estimate=pl.CostEstimate(flops=4 * SUB * tokens * tokens * width, transcendentals=SUB * tokens * tokens, bytes_accessed=12 * SUB * tokens * width),
        compiler_params=pltpu.CompilerParams(vmem_limit_bytes=LIMITS["inside"] * MIB),
        name="inside",
    )(log_decay, query_rows, kh, vh)


def output_kernel(tiled, head0, groups, *refs):
    intra, q2 = refs[:groups], refs[groups : 2 * groups]
    if tiled:
        near_ref, far_ref = refs[2 * groups : 2 * groups + 2]
        core, xbit = position()
        at = 2 * groups + 2
    else:
        state_ref = refs[2 * groups]
        at = 2 * groups + 1
    if head0:
        at += 1
    out_ref, flat, packed, sems = refs[at:]
    tokens = out_ref.shape[0]
    copies = []
    for g in range(groups):
        for i in range(SUB):
            slot = g * SUB + i
            if tiled:
                pieces = []
                for z in range(near_ref.shape[1]):
                    for x in range(2):
                        for c in range(2):
                            a = near_ref if c == 0 else far_ref
                            b = far_ref if c == 0 else near_ref
                            plain = jnp.where(core, b[x, z, slot], a[x, z, slot])
                            flipped = jnp.where(core, b[1 - x, z, slot], a[1 - x, z, slot])
                            pieces.append(jnp.where(xbit, flipped, plain))
                carried = jnp.concatenate(pieces, axis=0)
            else:
                carried = state_ref[slot]
            hi, low = split2(carried)
            right = jnp.concatenate([jnp.concatenate([hi, low], axis=1), jnp.concatenate([hi, jnp.zeros_like(low)], axis=1)], axis=0)
            both = jnp.dot(q2[g][i], right, preferred_element_type=F32)
            mixed = intra[g][i] + (both[:, :LANES] + both[:, LANES:])
            mean = jnp.mean(mixed * mixed, axis=1, keepdims=True)
            flat[pl.ds(i, tokens, stride=SUB), :] = mixed * lax.rsqrt(mean + norm_eps)
        packed[g] = flat[...].reshape(tokens, SUB, LANES).astype(BF16)
        copies.append(pltpu.make_async_copy(packed.at[g], out_ref.at[:, pl.ds(head0 + g * SUB, SUB), :], sems.at[g]))
        copies[-1].start()
    for copy in copies:
        copy.wait()


def outputs(tiled, heads, head0, insides, attended, *carried):
    groups = len(insides)
    intra, q2 = zip(*insides)
    _, tokens, width = intra[0].shape
    args = intra + q2 + carried
    specs = [VM] * len(args)
    alias = {}
    if head0:
        args += (attended,)
        specs.append(HBM)
        alias = {len(args) - 1: 0}
    return pl.pallas_call(
        functools.partial(output_kernel, tiled, head0, groups),
        in_specs=specs,
        out_specs=HBM,
        out_shape=jax.ShapeDtypeStruct((tokens, heads, width), BF16),
        scratch_shapes=[
            pltpu.VMEM((tokens * SUB, width), F32),
            pltpu.VMEM((groups, tokens, SUB, width), BF16),
            pltpu.SemaphoreType.DMA((groups,)),
        ],
        input_output_aliases=alias,
        cost_estimate=pl.CostEstimate(flops=4 * groups * SUB * tokens * width * width, transcendentals=2 * groups * SUB * tokens, bytes_accessed=8 * groups * SUB * tokens * width),
        compiler_params=pltpu.CompilerParams(vmem_limit_bytes=LIMITS["outputs"] * MIB),
        name="outputs",
    )(*args)


def decode_kernel(chunks, n, q_ref, k_ref, v_ref, d_ref, state_hbm, end_ref, near_ref, before_ref, qf, kf, vf, sbuf, sf, sems):
    steps, heads, width = q_ref.shape
    me = lax.axis_index("seq")
    block = lax.div(me, SUB)
    copies = []
    for c in range(chunks):
        start = pl.multiple_of(c * n + block * SUB, SUB)
        copies.append(pltpu.make_async_copy(state_hbm.at[:, pl.ds(start, SUB), :], sbuf.at[c], sems.at[c]))
        copies[-1].start()
    flatten(q_ref[...], qf)
    flatten(k_ref[...], kf)
    flatten(v_ref[...], vf)
    t = lax.broadcasted_iota(jnp.int32, (steps, LANES), 0)
    s = lax.broadcasted_iota(jnp.int32, (steps, LANES), 1)
    for c in range(chunks):
        head = c * n + me
        q, k, v = (f[pl.ds(head, steps, stride=heads), :] for f in (qf, kf, vf))
        lane = lax.broadcasted_iota(jnp.int32, (steps, heads), 1)
        own = jnp.sum(jnp.where(lane == head, d_ref[...], 0.0), axis=1, keepdims=True)
        order = lax.broadcasted_iota(jnp.int32, (steps, 1), 0)
        cum = jnp.zeros((steps, 1), F32)
        for u in range(steps):
            cum = cum + jnp.where(order >= u, own[u : u + 1], 0.0)
        column = jnp.broadcast_to(cum, (steps, LANES))
        row = jnp.sum(jnp.where(t == s, column, 0.0), axis=0, keepdims=True)
        pair = jnp.exp(jnp.where((t >= s) & (s < steps), column - row, -jnp.inf))
        end_ref[c] = jnp.exp(column)
        scores = lax.dot_general(q.astype(BF16), k.astype(BF16), (((1,), (1,)), ((), ())), preferred_element_type=F32)
        near = jnp.zeros((steps, width), F32)
        for u in range(steps):
            near = near + (scores[:, u : u + 1] * pair[:, u : u + 1]) * v[u : u + 1]
        near_ref[c] = near
        copies[c].wait()
        sf[...] = sbuf[c].reshape(width * SUB, width)
        state = sf[pl.ds(lax.rem(me, SUB), width, stride=SUB), :]
        before = None
        for piece in split3(state):
            part = jnp.dot(q.astype(BF16), piece, preferred_element_type=F32)
            before = part if before is None else before + part
        before_ref[c] = before


def decode_terms(chunks, n, decode_query, decode_key, decode_value, decode_decay, state_in):
    steps, heads, width = decode_query.shape
    out = jax.ShapeDtypeStruct((chunks, steps, width), F32)
    return pl.pallas_call(
        functools.partial(decode_kernel, chunks, n),
        in_specs=[VM] * 4 + [HBM],
        out_specs=[VM] * 3,
        out_shape=[out] * 3,
        scratch_shapes=[pltpu.VMEM((steps * heads, width), F32)] * 3
        + [
            pltpu.VMEM((chunks, width, SUB, width), F32),
            pltpu.VMEM((width * SUB, width), F32),
            pltpu.SemaphoreType.DMA((chunks,)),
        ],
        cost_estimate=pl.CostEstimate(flops=1 << 20, transcendentals=1 << 10, bytes_accessed=MIB),
        compiler_params=pltpu.CompilerParams(vmem_limit_bytes=LIMITS["decode"] * MIB),
        name="decode",
    )(decode_query, decode_key, decode_value, decode_decay, state_in)


def normalize(mixed):
    return mixed * lax.rsqrt(jnp.mean(mixed * mixed, axis=-1, keepdims=True) + norm_eps)


LIMITS = {"states": 24, "inside": 12, "outputs": 12, "decode": 4}


def local(query_rows, key_rows, value_rows, log_decay, state_in, decode_query, decode_key, decode_value, decode_decay):
    tokens, heads, width = query_rows.shape
    steps = decode_query.shape[0]
    n = lax.axis_size("seq")
    me = lax.axis_index("seq")
    spans = n // 4
    rows = width // n
    core, xbit, z = me % 2, (me // 2) % 2, me // 4
    tiled = rows % SUB == 0
    pseudo = tiled and rows == steps and heads % n == 0 and n % SUB == 0 and n * steps == width
    chunks = heads // n if pseudo else 1
    per = heads // chunks
    slots = per + (1 if pseudo else 0)

    swap_core = [(i, i ^ 1) for i in range(n)]
    swap_x = [(i, i ^ 2) for i in range(n)]
    shift = lambda s: [(i, (i + 4 * s) % n) for i in range(n)]

    def first(flag, a, b):
        return jnp.where(flag == 0, a, b)

    def weights(total, part):
        w = jnp.exp(total)[:, None, :]
        if pseudo:
            lead = part.shape[:-1]
            w = jnp.broadcast_to(w, lead + w.shape)
            w = jnp.concatenate([w, jnp.exp(part)[..., None, None, :]], axis=len(lead))
        return w

    def owners(total, x_rel):
        if not pseudo:
            return None
        t = total.reshape(spans, 2, 2, LANES)
        t = lax.dynamic_index_in_dim(t, core, 2, keepdims=False)
        return lax.dynamic_index_in_dim(t, (xbit + x_rel) % 2, 1, keepdims=False)

    def swap(flat, shape, count, pairs):
        got = lax.ppermute(flat, "seq", pairs)
        return got[:-count].reshape(shape), got[-count:]

    def exchange(x, total, pairs):
        flat = jnp.concatenate([x.reshape(-1, width), total], axis=0)
        return swap(flat, x.shape, total.shape[0], pairs)

    def to_absolute(pieces):
        turned = jnp.stack(pieces[::-1] + pieces[:0:-1])
        return lax.dynamic_slice_in_dim(turned, spans - 1 - z, spans, 0)

    kept, by_head = [], []
    left = None
    for c in range(chunks):
        if c == 0:
            made = states(c, per, tiled, pseudo, rows, spans, (log_decay, decode_query, key_rows, value_rows))
            left = made[5:]
        else:
            made = states(c, per, tiled, pseudo, rows, spans, (left[0], left[1], decode_query, left[2], left[3]))
        keep, send, total, kh, vh = made[:5]
        if not tiled:
            parts = jnp.transpose(keep.reshape(per, spans, 2, 2, rows, width), (3, 2, 1, 0, 4, 5))
            parts = jnp.where(xbit == 0, parts, parts[:, ::-1])
            keep, send = first(core, parts[0], parts[1]), first(core, parts[1], parts[0])
            send = jnp.concatenate([send.reshape(-1, width), total], axis=0)
        kept.append((keep, send, total))
        by_head.append((kh, vh))

    groups = per // SUB
    insides = [
        [inside_block(c * groups + g, g * SUB, log_decay, query_rows, *by_head[c]) for g in range(groups)]
        for c in range(chunks)
    ]
    if pseudo:
        from_end, near, before = decode_terms(chunks, n, decode_query, decode_key, decode_value, decode_decay, state_in)
    prior = jnp.transpose(lax.dynamic_slice_in_dim(state_in, me * rows, rows, 0), (1, 0, 2))

    level = []
    for c in range(chunks):
        keep, send, total = kept[c]
        got, got_total = swap(send, keep.shape, per, swap_core)
        part = lambda t: jnp.stack([owners(t, 0), owners(t, 1)]) if pseudo else None
        mine = first(core, weights(got_total, part(got_total)), 1.0)
        theirs = first(core, 1.0, weights(total, part(total)))
        chip = keep * mine + got * theirs
        chip_total = total + got_total
        got_x, got_x_total = exchange(chip[1], chip_total, swap_x)
        mine = first(xbit, weights(got_x_total, owners(got_x_total, 0)), 1.0)
        theirs = first(xbit, 1.0, weights(chip_total, owners(chip_total, 0)))
        span = chip[0] * mine + got_x * theirs
        level.append((got, got_total, chip, chip_total, got_x, got_x_total, span, chip_total + got_x_total))

    finals, carries = [], []
    for c in range(chunks):
        span, span_total = level[c][6:]
        pieces = [lax.dynamic_index_in_dim(span, z, 0, keepdims=False)]
        totals = [span_total]
        for s in range(1, spans):
            piece, t = exchange(lax.dynamic_index_in_dim(span, (z + s) % spans, 0, keepdims=False), span_total, shift(s))
            pieces.append(piece)
            totals.append(t)
        pieces, totals = to_absolute(pieces), to_absolute(totals)
        carried = prior[c * per : (c + 1) * per]
        if pseudo:
            carried = jnp.concatenate([carried, before[c][None]], axis=0)
        all_carried = []
        for s in range(spans):
            all_carried.append(carried)
            t = totals[s]
            own = lax.dynamic_index_in_dim(t, me, 0, keepdims=False) if pseudo else None
            carried = carried * weights(t, own) + pieces[s]
        finals.append(carried[:per])
        if pseudo:
            dec = normalize(carried[per] * from_end[c] + near[c])
            all_carried = [jnp.concatenate([a[:per], dec[None]], axis=0) for a in all_carried]
        all_carried = jnp.stack(all_carried)
        pieces = [lax.dynamic_index_in_dim(all_carried, z, 0, keepdims=False)]
        for s in range(1, spans):
            pieces.append(lax.ppermute(lax.dynamic_index_in_dim(all_carried, (z + s) % spans, 0, keepdims=False), "seq", shift(s)))
        carries.append(to_absolute(pieces))

    slot = lax.broadcasted_iota(jnp.int32, (slots, 1, 1), 0)

    def advance(carried, total, state):
        w = jnp.exp(total)[:, None, :]
        if not pseudo:
            return carried * w + state
        w = jnp.concatenate([w, jnp.ones((1, 1, LANES), F32)], axis=0)
        return carried * w + jnp.where(slot < per, state, 0.0)

    attended, dec_out = None, []
    for c in range(chunks):
        keep, send, total = kept[c]
        got, got_total, chip, chip_total, got_x, got_x_total, _, _ = level[c]
        at_span = carries[c]
        msg = first(xbit, advance(at_span, chip_total, chip[0]), at_span)
        own = first(xbit, at_span, advance(at_span, got_x_total, got_x))
        at_chip = jnp.stack([own, lax.ppermute(msg, "seq", swap_x)])
        msg = first(core, advance(at_chip, total, keep), at_chip)
        own = first(core, at_chip, advance(at_chip, got_total, got))
        other = lax.ppermute(msg, "seq", swap_core)
        if tiled:
            carried = (own, other)
        else:
            both = jnp.stack([first(core, own, other), first(core, other, own)])
            both = jnp.where(xbit == 0, both, both[:, ::-1])
            carried = (jnp.transpose(both, (3, 2, 1, 0, 4, 5)).reshape(per, width, width),)
        attended = outputs(tiled, heads, c * per, insides[c], attended, *carried)
        if pseudo:
            both = jnp.stack([first(core, own[:, :, per], other[:, :, per]), first(core, other[:, :, per], own[:, :, per])])
            both = jnp.where(xbit == 0, both, both[:, ::-1])
            dec_out.append(jnp.transpose(both, (3, 2, 1, 0, 4)).reshape(steps, per, width))

    final_rows = jnp.transpose(jnp.concatenate(finals, axis=0), (1, 0, 2))
    if pseudo:
        decode_out = jnp.concatenate(dec_out, axis=1)
    else:
        start = me * rows
        key_part = lax.dynamic_slice_in_dim(decode_key, start, rows, 2).astype(F32)
        query_part = lax.dynamic_slice_in_dim(decode_query, start, rows, 2).astype(F32)
        order = jnp.arange(steps)
        causal = order[:, None, None] >= order[None, :, None]
        cum = jnp.cumsum(decode_decay, axis=0)
        pair = jnp.exp(jnp.where(causal, cum[:, None] - cum[None, :], -jnp.inf))
        scores = jnp.einsum("thr,shr->tsh", query_part, key_part, precision=HIGH) * pair
        inside = jnp.einsum("tsh,she->the", scores, decode_value.astype(F32), precision=HIGH)
        far = jnp.einsum("thr,rhe->the", query_part, final_rows, precision=HIGH) * jnp.exp(cum)[:, :, None]
        decode_out = normalize(lax.psum(inside + far, "seq"))
    return attended, final_rows, decode_out


def solution(mesh):
    in_specs = (
        P("seq", "head", None),
        P("seq", "head", None),
        P("seq", "head", None),
        P("seq", "head"),
        P(None, "head", None),
        P(None, "head", None),
        P(None, "head", None),
        P(None, "head", None),
        P(None, "head"),
    )
    out_specs = (P("seq", "head", None), P("seq", "head", None), P(None, "head", None))
    return jax.shard_map(local, mesh=mesh, in_specs=in_specs, out_specs=out_specs, check_vma=False)
```

time: 135 us -> 128 us (0.948)
  waiting for transfers between devices: 20.7 us -> 39.2 us
  Pallas kernels: 55.8 us -> 37.6 us
  local copies, waits for them, and re-layouts: 12.8 us -> 20.4 us
  starting transfers between devices: 28.8 us -> 21.9 us
  matrix products: 4.66 us -> 0 us
  other arithmetic: 9.57 us -> 5.95 us
    pallas_call x6 -> x9, Pallas kernels: 55.8 us -> 37.6 us  [the longest x4 19.5 us: inside_block(): pl.pallas_call(functools.partial(inside_kernel, 128, group * SUB, slot0),...]
    unnamed x64 -> x76, local copies, waits for them, and re-layouts: 3.29 us -> 15.4 us
    ppermute x10, waiting for transfers between devices: 9.93 us -> 18.9 us  [swap(): got = lax.ppermute(flat, 'seq', pairs)]
    ppermute x2, waiting for transfers between devices: 4.63 us -> 11.2 us  [local(): at_chip = jnp.stack([own, lax.ppermute(msg, 'seq', swap_x)])]
    dot_general x6 -> x0, matrix products: 4.66 us -> none  [the longest x4 2.66 us: local(): near = jnp.dot(jnp.dot(q, k.T, precision=HIGH) * pair, v, precision=HIGH)]
    concatenate x1 -> x0, other arithmetic: 4.32 us -> none  [local(): attended = jnp.concatenate(attended, axis=1)]
    dynamic_slice x5 -> x0, local copies, waits for them, and re-layouts: 4.14 us -> none  [the longest x4 4.11 us: own_head(): return lax.dynamic_index_in_dim(x, c * n + me, axis, keepdims=False)]
    ppermute x10, starting transfers between devices: 16.4 us -> 12.6 us  [swap(): got = lax.ppermute(flat, 'seq', pairs)]
  transfers between devices with their start and end apart: 20 -> 20, of which waited for: 7 -> 10; matrix products, arithmetic and copies ran while one was open for 13% -> 9% of each run, Pallas kernels for 24% -> 16%
where the time goes in v1:
time: 128 us; the launch traced here: 127 us
  waiting for transfers between devices  39.2 us (31%)
  Pallas kernels  37.6 us (29%)
  starting transfers between devices  21.9 us (17%)
  local copies, waits for them, and re-layouts  20.4 us (16%)
  other arithmetic  5.95 us (5%)
  between operations  1.94 us (2%)
    pallas_call x4, Pallas kernels, inside_block(): pl.pallas_call(functools.partial(inside_kernel, 128, group * SUB, slot0),...  19.5 us
    ppermute x10, waiting for transfers between devices, swap(): got = lax.ppermute(flat, 'seq', pairs)  18.9 us
    unnamed x76, local copies, waits for them, and re-layouts  15.4 us
    ppermute x10, starting transfers between devices, swap(): got = lax.ppermute(flat, 'seq', pairs)  12.6 us
    ppermute x2, waiting for transfers between devices, local(): at_chip = jnp.stack([own, lax.ppermute(msg, 'seq', swap_x)])  11.2 us
    pallas_call x2, Pallas kernels, states(): pl.pallas_call(functools.partial(state_kernel, tiled, pseudo, rows, per,...  11.1 us
    ppermute x6, waiting for transfers between devices, local(): lax.ppermute(lax.dynamic_index_in_dim(all_carried, (z + s) % spans, 0, ke...  7.23 us
    ppermute x6, starting transfers between devices, local(): lax.ppermute(lax.dynamic_index_in_dim(all_carried, (z + s) % spans, 0, ke...  7.08 us
  transfers between devices with their start and end apart: 20, of which 10 were waited for; matrix products, arithmetic and copies ran while one was open for 9% of the time, Pallas kernels for 16%

profile of v1, /device:TPU:0, one launch (start us, length us, event | category | flops | bytes accessed | tf_op | source)
XLA Modules:
  0.0 127.0 jit_solution(7485375210997707437)
XLA Ops:
  1.6 2.2 %copy-done.7 = bf16[512,32,128]{2,1,0:T(8,128)(2,1)S(1)} copy-done((bf16[512,32,128]{2,1,0:T(8,128)(2,1)S(1)}, bf16[512,32,128]{2,1,0:T(8,128)(2,1)}, u32[]{:S(2)}) %copy-start.7) | copy-done | bytes 4194328
  3.8 2.2 %copy-done.8 = bf16[512,32,128]{2,1,0:T(8,128)(2,1)S(1)} copy-done((bf16[512,32,128]{2,1,0:T(8,128)(2,1)S(1)}, bf16[512,32,128]{2,1,0:T(8,128)(2,1)}, u32[]{:S(2)}) %copy-start.8) | copy-done | bytes 4194328
  6.8 6.5 %states.2 = (f32[2,4,17,8,128]{4,3,2,1,0:T(8,128)S(1)}, f32[1104,128]{1,0:T(8,128)}, f32[16,128]{1,0:T(8,128)S(1)}, bf16[16,512,128]{2,1,0:T(8,128)(2,1)S(1)}, b...) custom-call(f32[512,32]{1,0:T(8,128)S(1)} %copy.110.refs_0_.ld_ref, ...), custom_call_target="tpu_custom_call" | custom-call | flops 536870912 | bytes 4194304 | tf_op jit(solution)/shard_map/states/pallas_call | solution.py:204
  13.3 4.6 %states.3 = (f32[2,4,17,8,128]{4,3,2,1,0:T(8,128)S(1)}, f32[1104,128]{1,0:T(8,128)}, f32[16,128]{1,0:T(8,128)S(1)}, bf16[16,512,128]{2,1,0:T(8,128)(2,1)S(1)}, bf16[16,512,128]{2,1,0:T(8,128)(2,1)S(1)}) custom-call(f32[512,32]{1,0:T(8,128)S(1)} %get-tuple-element.28.refs_0_, f32[32,128]{1,0:T(8,128)S(1)} %get-tuple-element.29.refs_1_, ...), custom_call_target="tpu_custom_call" | custom-call | flops 536870912 | bytes 4194304 | tf_op jit(solution)/shard_map/states/pallas_call | solution.py:204
  32.2 3.0 %collective-permute-start.1 = (f32[560,128]{1,0:T(8,128)S(1)}, f32[560,128]{1,0:T(8,128)S(1)}, u32[]{:S(2)}, u32[]{:S(2)}) collective-permute-start(f32[560,128]{1,0:T(8,128)S(1)} %pad_maximum_fusion.2), channel_id=1, source_target_pairs={{0,4},{2,6},{4,0},{6,2},{8,12},{10,14},{12,8},{14,10},{16,20},{18,... | collective-permute-start | bytes 860168 | tf_op jit(solution)/shard_map/ppermute | solution.py:440
  37.6 5.4 %collective-permute-done.1 = f32[560,128]{1,0:T(8,128)S(1)} collective-permute-done((f32[560,128]{1,0:T(8,128)S(1)}, f32[560,128]{1,0:T(8,128)S(1)}, u32[]{:S(2)}, u32[]{:S(2)}) %collective-permute-start.1) | collective-permute-done | bytes 286752 | tf_op jit(solution)/shard_map/ppermute | solution.py:440
  42.9 5.5 %collective-permute-done.11 = f32[560,128]{1,0:T(8,128)S(1)} collective-permute-done((f32[560,128]{1,0:T(8,128)S(1)}, f32[560,128]{1,0:T(8,128)S(1)}, u32[]{:S(2)}, u32[]{:S(2)}) %collective-permute-start.11) | collective-permute-done | bytes 286752 | tf_op jit(solution)/shard_map/ppermute | solution.py:440
  48.7 3.9 %collective-permute-start.2 = (f32[152,128]{1,0:T(8,128)S(1)}, f32[152,128]{1,0:T(8,128)S(1)}, u32[]{:S(2)}, u32[]{:S(2)}) collective-permute-start(f32[152,128]{1,0:T(8,128)S(1)} %get-tuple-element.150), channel_id=1, source_target_pairs={{0,24},{2,26},{4,28},{6,30},{8,0},{10,2},{12,4},{14,6},{16,8},{18,... | collective-permute-start | bytes 233480 | tf_op jit(solution)/shard_map/ppermute | solution.py:440
  53.8 2.9 %collective-permute-start.12 = (f32[152,128]{1,0:T(8,128)S(1)}, f32[152,128]{1,0:T(8,128)S(1)}, u32[]{:S(2)}, u32[]{:S(2)}) collective-permute-start(f32[152,128]{1,0:T(8,128)S(1)} %get-tuple-element.153), channel_id=1, source_target_pairs={{0,24},{2,26},{4,28},{6,30},{8,0},{10,2},{12,4},{14,6},{16,8},{18,... | collective-permute-start | bytes 233480 | tf_op jit(solution)/shard_map/ppermute | solution.py:440
  57.8 4.3 %collective-permute-done.3 = f32[152,128]{1,0:T(8,128)S(1)} collective-permute-done((f32[152,128]{1,0:T(8,128)S(1)}, f32[152,128]{1,0:T(8,128)S(1)}, u32[]{:S(2)}, u32[]{:S(2)}) %collective-permute-start.3) | collective-permute-done | bytes 77856 | tf_op jit(solution)/shard_map/ppermute | solution.py:440
  62.3 3.8 %collective-permute-done.13 = f32[152,128]{1,0:T(8,128)S(1)} collective-permute-done((f32[152,128]{1,0:T(8,128)S(1)}, f32[152,128]{1,0:T(8,128)S(1)}, u32[]{:S(2)}, u32[]{:S(2)}) %collective-permute-start.13) | collective-permute-done | bytes 77856 | tf_op jit(solution)/shard_map/ppermute | solution.py:440
  67.0 1.9 %collective-permute-start.5 = (f32[17,8,128]{2,1,0:T(8,128)S(1)}, f32[17,8,128]{2,1,0:T(8,128)S(1)}, u32[]{:S(2)}, u32[]{:S(2)}) collective-permute-start(f32[17,8,128]{2,1,0:T(8,128)S(1)} %get-tuple-element.113), channel_id=1, source_target_pairs={{0,24},{2,26},{4,28},{6,30},{8,0},{10,2},{12,4},{14,6},{16,8},{18,... | collective-permute-start | bytes 208904 | tf_op jit(solution)/shard_map/ppermute | solution.py:518
  68.9 1.9 %collective-permute-start.7 = (f32[17,8,128]{2,1,0:T(8,128)S(1)}, f32[17,8,128]{2,1,0:T(8,128)S(1)}, u32[]{:S(2)}, u32[]{:S(2)}) collective-permute-start(f32[17,8,128]{2,1,0:T(8,128)S(1)} %get-tuple-element.111), channel_id=1, source_target_pairs={{0,8},{2,10},{4,12},{6,14},{8,16},{10,18},{12,20},{14,22},{16,24},... | collective-permute-start | bytes 208904 | tf_op jit(solution)/shard_map/ppermute | solution.py:518
  70.9 2.0 %collective-permute-start.15 = (f32[17,8,128]{2,1,0:T(8,128)S(1)}, f32[17,8,128]{2,1,0:T(8,128)S(1)}, u32[]{:S(2)}, u32[]{:S(2)}) collective-permute-start(f32[17,8,128]{2,1,0:T(8,128)S(1)} %get-tuple-element.110), channel_id=1, source_target_pairs={{0,24},{2,26},{4,28},{6,30},{8,0},{10,2},{12,4},{14,6},{16,8},{18,... | collective-permute-start | bytes 208904 | tf_op jit(solution)/shard_map/ppermute | solution.py:518
  74.3 2.5 %collective-permute-done.15 = f32[17,8,128]{2,1,0:T(8,128)S(1)} collective-permute-done((f32[17,8,128]{2,1,0:T(8,128)S(1)}, f32[17,8,128]{2,1,0:T(8,128)S(1)}, u32[]{:S(2)}, u32[]{:S(2)}) %collective-permute-start.15) | collective-permute-done | bytes 69664 | tf_op jit(solution)/shard_map/ppermute | solution.py:518
  77.8 3.8 %collective-permute-done.16 = f32[17,8,128]{2,1,0:T(8,128)S(1)} collective-permute-done((f32[17,8,128]{2,1,0:T(8,128)S(1)}, f32[17,8,128]{2,1,0:T(8,128)S(1)}, u32[]{:S(2)}, u32[]{:S(2)}) %collective-permute-start.16) | collective-permute-done | bytes 69664 | tf_op jit(solution)/shard_map/ppermute | solution.py:518
  84.0 7.5 %collective-permute-done.18 = f32[4,17,8,128]{3,2,0,1:T(8,128)S(1)} collective-permute-done((f32[4,17,8,128]{3,2,0,1:T(8,128)S(1)}, f32[4,17,8,128]{3,2,0,1:T(8,128)S(1)}, u32[]{:S(2)}, u32[]{:S(2)}) %collective-permute-start.18) | collective-permute-done | bytes 278560 | tf_op jit(solution)/shard_map/ppermute | solution.py:537
  91.5 3.8 %collective-permute-done.8 = f32[4,17,8,128]{3,2,0,1:T(8,128)S(1)} collective-permute-done((f32[4,17,8,128]{3,2,0,1:T(8,128)S(1)}, f32[4,17,8,128]{3,2,0,1:T(8,128)S(1)}, u32[]{:S(2)}, u32[]{:S(2)}) %collective-permute-start.8) | collective-permute-done | bytes 278560 | tf_op jit(solution)/shard_map/ppermute | solution.py:537
  97.5 4.6 %inside.6 = (f32[8,512,128]{2,1,0:T(8,128)S(1)}, bf16[8,512,256]{2,1,0:T(8,128)(2,1)S(1)}) custom-call(f32[512,32]{1,0:T(8,128)S(1)} %copy.110.refs_0_.ld_ref, bf16[512,32,128]{2,1,0:T(8,128)(2,1)S(1)} %copy-done, bf16[16,512,128]{2,1,0:T(8,128)(2,1)S(1)} %copy-done.4, bf16[16,512,128]{2,1,0:T(8,128)(2,1)S(1)} %copy-done.6), custom_call_target="tpu_custom_call" | custom-call | flops 1073741824 | bytes 6291456 | tf_op jit(solution)/shard_map/inside/pallas_call | solution.py:248
  102.1 4.9 %inside.7 = (f32[8,512,128]{2,1,0:T(8,128)S(1)}, bf16[8,512,256]{2,1,0:T(8,128)(2,1)S(1)}) custom-call(f32[512,32]{1,0:T(8,128)S(1)} %copy.110.refs_0_.ld_ref, bf16[512,32,128]{2,1,0:T(8,128)(2,1)S(1)} %copy-done, bf16[16,512,128]{2,1,0:T(8,128)(2,1)S(1)} %copy-done.4, bf16[16,512,128]{2,1,0:T(8,128)(2,1)S(1)} %copy-done.6), custom_call_target="tpu_custom_call" | custom-call | flops 1073741824 | bytes 6291456 | tf_op jit(solution)/shard_map/inside/pallas_call | solution.py:248
  107.0 5.1 %inside.5 = (f32[8,512,128]{2,1,0:T(8,128)S(1)}, bf16[8,512,256]{2,1,0:T(8,128)(2,1)S(1)}) custom-call(f32[512,32]{1,0:T(8,128)S(1)} %copy.110.refs_0_.ld_ref, bf16[512,32,128]{2,1,0:T(8,128)(2,1)S(1)} %copy-done, bf16[16,512,128]{2,1,0:T(8,128)(2,1)S(1)} %get-tuple-element.32.kh_ref, bf16[16,512,128]{2,1,0:T(8,128)(2,1)S(1)} %copy-done.2), custom_call_target="tpu_custom_call" | custom-call | flops 1073741824 | bytes 6291456 | tf_op jit(solution)/shard_map/inside/pallas_call | solution.py:248
  112.1 4.9 %inside.4 = (f32[8,512,128]{2,1,0:T(8,128)S(1)}, bf16[8,512,256]{2,1,0:T(8,128)(2,1)S(1)}) custom-call(f32[512,32]{1,0:T(8,128)S(1)} %copy.110.refs_0_.ld_ref, bf16[512,32,128]{2,1,0:T(8,128)(2,1)S(1)} %copy-done, bf16[16,512,128]{2,1,0:T(8,128)(2,1)S(1)} %get-tuple-element.32.kh_ref, bf16[16,512,128]{2,1,0:T(8,128)(2,1)S(1)} %copy-done.2), custom_call_target="tpu_custom_call" | custom-call | flops 1073741824 | bytes 6291456 | tf_op jit(solution)/shard_map/inside/pallas_call | solution.py:248
  120.7 3.0 %outputs.2.refs_6_ = bf16[512,32,128]{2,1,0:T(8,128)(2,1)} custom-call(f32[8,512,128]{2,1,0:T(8,128)S(1)} %get-tuple-element.46.refs_0_, f32[8,512,128]{2,1,0:T(8,128)S(1)} %get-tuple-element.47.refs_1_, bf16[8,512,256]{2,1,0:T(8,128)(2,1)S(1)} %get-tuple-element.48.refs_2_, bf16[8,512,256]{2,1,0:T(8,128)(2,1)S(1)} %get-tuple-element.49.refs_3_, ...), custom_call_target="tpu_custom_call" | custom-call | flops 536870912 | bytes 8388608 | tf_op jit(solution)/shard_map/outputs/pallas_call | solution.py:317
  123.7 3.1 %outputs.3 = bf16[512,32,128]{2,1,0:T(8,128)(2,1)} custom-call(f32[8,512,128]{2,1,0:T(8,128)S(1)} %get-tuple-element.34.refs_0_, f32[8,512,128]{2,1,0:T(8,128)S(1)} %get-tuple-element.35.refs_1_, bf16[8,512,256]{2,1,0:T(8,128)(2,1)S(1)} %get-tuple-element.36.refs_2_, ...), custom_call_target="tpu_custom_call", output_to_operand_aliasing={{}: (6, {})} | custom-call | flops 536870912 | bytes 8388608 | tf_op jit(solution)/shard_map/outputs/pallas_call | solution.py:317
  (215 shorter events, 32.0 us)
Async XLA Ops:
  13.3 11.8 %copy-start.11 = (bf16[8,32,128]{2,1,0:T(8,128)(2,1)S(1)}, bf16[8,32,128]{2,1,0:T(8,128)(2,1)}, u32[]{:S(2)}) copy-start(bf16[8,32,128]{2,1,0:T(8,128)(2,1)} %q_ref.7) | copy-start | bytes 196612
  19.2 10.8 %collective-permute-start = (f32[1104,128]{1,0:T(8,128)}, f32[1104,128]{1,0:T(8,128)}, u32[]{:S(2)}, u32[]{:S(2)}) collective-permute-start(f32[1104,128]{1,0:T(8,128)} %get-tuple-element.40), channel_id=1, source_target_pairs={{0,2},{2,0},{4,6},{6,4},{8,10},{10,8},{12,14},{14,12},{16,18},{18,... | collective-permute-start | bytes 1695752 | tf_op jit(solution)/shard_map/ppermute | solution.py:440
  19.7 15.5 %collective-permute-start.10 = (f32[1104,128]{1,0:T(8,128)}, f32[1104,128]{1,0:T(8,128)}, u32[]{:S(2)}, u32[]{:S(2)}) collective-permute-start(f32[1104,128]{1,0:T(8,128)} %get-tuple-element.51), channel_id=1, source_target_pairs={{0,2},{2,0},{4,6},{6,4},{8,10},{10,8},{12,14},{14,12},{16,18},{18,... | collective-permute-start | bytes 1695752 | tf_op jit(solution)/shard_map/ppermute | solution.py:440
  32.2 10.7 %collective-permute-start.1 = (f32[560,128]{1,0:T(8,128)S(1)}, f32[560,128]{1,0:T(8,128)S(1)}, u32[]{:S(2)}, u32[]{:S(2)}) collective-permute-start(f32[560,128]{1,0:T(8,128)S(1)} %pad_maximum_fusion.2), channel_id=1, source_target_pairs={{0,4},{2,6},{4,0},{6,2},{8,12},{10,14},{12,8},{14,10},{16,20},{18,... | collective-permute-start | bytes 860168 | tf_op jit(solution)/shard_map/ppermute | solution.py:440
  37.4 11.0 %collective-permute-start.11 = (f32[560,128]{1,0:T(8,128)S(1)}, f32[560,128]{1,0:T(8,128)S(1)}, u32[]{:S(2)}, u32[]{:S(2)}) collective-permute-start(f32[560,128]{1,0:T(8,128)S(1)} %pad_maximum_fusion.3), channel_id=1, source_target_pairs={{0,4},{2,6},{4,0},{6,2},{8,12},{10,14},{12,8},{14,10},{16,20},{18,... | collective-permute-start | bytes 860168 | tf_op jit(solution)/shard_map/ppermute | solution.py:440
  48.7 9.1 %collective-permute-start.2 = (f32[152,128]{1,0:T(8,128)S(1)}, f32[152,128]{1,0:T(8,128)S(1)}, u32[]{:S(2)}, u32[]{:S(2)}) collective-permute-start(f32[152,128]{1,0:T(8,128)S(1)} %get-tuple-element.150), channel_id=1, source_target_pairs={{0,24},{2,26},{4,28},{6,30},{8,0},{10,2},{12,4},{14,6},{16,8},{18,... | collective-permute-start | bytes 233480 | tf_op jit(solution)/shard_map/ppermute | solution.py:440
  52.6 9.6 %collective-permute-start.3 = (f32[152,128]{1,0:T(8,128)S(1)}, f32[152,128]{1,0:T(8,128)S(1)}, u32[]{:S(2)}, u32[]{:S(2)}) collective-permute-start(f32[152,128]{1,0:T(8,128)S(1)} %get-tuple-element.149), channel_id=1, source_target_pairs={{0,16},{2,18},{4,20},{6,22},{8,24},{10,26},{12,28},{14,30},{16,0},... | collective-permute-start | bytes 233480 | tf_op jit(solution)/shard_map/ppermute | solution.py:440
  52.6 9.6 %collective-permute-start.4 = (f32[152,128]{1,0:T(8,128)S(1)}, f32[152,128]{1,0:T(8,128)S(1)}, u32[]{:S(2)}, u32[]{:S(2)}) collective-permute-start(f32[152,128]{1,0:T(8,128)S(1)} %get-tuple-element.148), channel_id=1, source_target_pairs={{0,8},{2,10},{4,12},{6,14},{8,16},{10,18},{12,20},{14,22},{16,24},... | collective-permute-start | bytes 233480 | tf_op jit(solution)/shard_map/ppermute | solution.py:440
  53.8 8.5 %collective-permute-start.12 = (f32[152,128]{1,0:T(8,128)S(1)}, f32[152,128]{1,0:T(8,128)S(1)}, u32[]{:S(2)}, u32[]{:S(2)}) collective-permute-start(f32[152,128]{1,0:T(8,128)S(1)} %get-tuple-element.153), channel_id=1, source_target_pairs={{0,24},{2,26},{4,28},{6,30},{8,0},{10,2},{12,4},{14,6},{16,8},{18,... | collective-permute-start | bytes 233480 | tf_op jit(solution)/shard_map/ppermute | solution.py:440
  56.6 9.4 %collective-permute-start.13 = (f32[152,128]{1,0:T(8,128)S(1)}, f32[152,128]{1,0:T(8,128)S(1)}, u32[]{:S(2)}, u32[]{:S(2)}) collective-permute-start(f32[152,128]{1,0:T(8,128)S(1)} %get-tuple-element.152), channel_id=1, source_target_pairs={{0,16},{2,18},{4,20},{6,22},{8,24},{10,26},{12,28},{14,30},{16,0},... | collective-permute-start | bytes 233480 | tf_op jit(solution)/shard_map/ppermute | solution.py:440
  57.8 8.3 %collective-permute-start.14 = (f32[152,128]{1,0:T(8,128)S(1)}, f32[152,128]{1,0:T(8,128)S(1)}, u32[]{:S(2)}, u32[]{:S(2)}) collective-permute-start(f32[152,128]{1,0:T(8,128)S(1)} %get-tuple-element.151), channel_id=1, source_target_pairs={{0,8},{2,10},{4,12},{6,14},{8,16},{10,18},{12,20},{14,22},{16,24},... | collective-permute-start | bytes 233480 | tf_op jit(solution)/shard_map/ppermute | solution.py:440
  67.0 7.0 %collective-permute-start.5 = (f32[17,8,128]{2,1,0:T(8,128)S(1)}, f32[17,8,128]{2,1,0:T(8,128)S(1)}, u32[]{:S(2)}, u32[]{:S(2)}) collective-permute-start(f32[17,8,128]{2,1,0:T(8,128)S(1)} %get-tuple-element.113), channel_id=1, source_target_pairs={{0,24},{2,26},{4,28},{6,30},{8,0},{10,2},{12,4},{14,6},{16,8},{18,... | collective-permute-start | bytes 208904 | tf_op jit(solution)/shard_map/ppermute | solution.py:518
  68.9 8.8 %collective-permute-start.6 = (f32[17,8,128]{2,1,0:T(8,128)S(1)}, f32[17,8,128]{2,1,0:T(8,128)S(1)}, u32[]{:S(2)}, u32[]{:S(2)}) collective-permute-start(f32[17,8,128]{2,1,0:T(8,128)S(1)} %get-tuple-element.112), channel_id=1, source_target_pairs={{0,16},{2,18},{4,20},{6,22},{8,24},{10,26},{12,28},{14,30},{16,0},... | collective-permute-start | bytes 208904 | tf_op jit(solution)/shard_map/ppermute | solution.py:518
  68.9 8.8 %collective-permute-start.7 = (f32[17,8,128]{2,1,0:T(8,128)S(1)}, f32[17,8,128]{2,1,0:T(8,128)S(1)}, u32[]{:S(2)}, u32[]{:S(2)}) collective-permute-start(f32[17,8,128]{2,1,0:T(8,128)S(1)} %get-tuple-element.111), channel_id=1, source_target_pairs={{0,8},{2,10},{4,12},{6,14},{8,16},{10,18},{12,20},{14,22},{16,24},... | collective-permute-start | bytes 208904 | tf_op jit(solution)/shard_map/ppermute | solution.py:518
  70.9 5.8 %collective-permute-start.15 = (f32[17,8,128]{2,1,0:T(8,128)S(1)}, f32[17,8,128]{2,1,0:T(8,128)S(1)}, u32[]{:S(2)}, u32[]{:S(2)}) collective-permute-start(f32[17,8,128]{2,1,0:T(8,128)S(1)} %get-tuple-element.110), channel_id=1, source_target_pairs={{0,24},{2,26},{4,28},{6,30},{8,0},{10,2},{12,4},{14,6},{16,8},{18,... | collective-permute-start | bytes 208904 | tf_op jit(solution)/shard_map/ppermute | solution.py:518
  72.9 8.6 %collective-permute-start.16 = (f32[17,8,128]{2,1,0:T(8,128)S(1)}, f32[17,8,128]{2,1,0:T(8,128)S(1)}, u32[]{:S(2)}, u32[]{:S(2)}) collective-permute-start(f32[17,8,128]{2,1,0:T(8,128)S(1)} %get-tuple-element.109), channel_id=1, source_target_pairs={{0,16},{2,18},{4,20},{6,22},{8,24},{10,26},{12,28},{14,30},{16,0},... | collective-permute-start | bytes 208904 | tf_op jit(solution)/shard_map/ppermute | solution.py:518
  74.0 7.5 %collective-permute-start.17 = (f32[17,8,128]{2,1,0:T(8,128)S(1)}, f32[17,8,128]{2,1,0:T(8,128)S(1)}, u32[]{:S(2)}, u32[]{:S(2)}) collective-permute-start(f32[17,8,128]{2,1,0:T(8,128)S(1)} %get-tuple-element.108), channel_id=1, source_target_pairs={{0,8},{2,10},{4,12},{6,14},{8,16},{10,18},{12,20},{14,22},{16,24},... | collective-permute-start | bytes 208904 | tf_op jit(solution)/shard_map/ppermute | solution.py:518
  81.7 14.2 %copy-start.4 = (bf16[16,512,128]{2,1,0:T(8,128)(2,1)S(1)}, bf16[16,512,128]{2,1,0:T(8,128)(2,1)}, u32[]{:S(2)}) copy-start(bf16[16,512,128]{2,1,0:T(8,128)(2,1)} %copy-done.3) | copy-start | bytes 6291460
  81.7 14.2 %copy-start.6 = (bf16[16,512,128]{2,1,0:T(8,128)(2,1)S(1)}, bf16[16,512,128]{2,1,0:T(8,128)(2,1)}, u32[]{:S(2)}) copy-start(bf16[16,512,128]{2,1,0:T(8,128)(2,1)} %copy-done.5) | copy-start | bytes 6291460
  81.9 9.6 %collective-permute-start.18 = (f32[4,17,8,128]{3,2,0,1:T(8,128)S(1)}, f32[4,17,8,128]{3,2,0,1:T(8,128)S(1)}, u32[]{:S(2)}, u32[]{:S(2)}) collective-permute-start(f32[4,17,8,128]{3,2,0,1:T(8,128)S(1)} %get-tuple-element.97), channel_id=1, source_target_pairs={{0,4},{2,6},{4,0},{6,2},{8,12},{10,14},{12,8},{14,10},{16,20},{18,... | collective-permute-start | bytes 835592 | tf_op jit(solution)/shard_map/ppermute | solution.py:537
  83.5 11.8 %collective-permute-start.8 = (f32[4,17,8,128]{3,2,0,1:T(8,128)S(1)}, f32[4,17,8,128]{3,2,0,1:T(8,128)S(1)}, u32[]{:S(2)}, u32[]{:S(2)}) collective-permute-start(f32[4,17,8,128]{3,2,0,1:T(8,128)S(1)} %get-tuple-element.172), channel_id=1, source_target_pairs={{0,4},{2,6},{4,0},{6,2},{8,12},{10,14},{12,8},{14,10},{16,20},{18,... | collective-permute-start | bytes 835592 | tf_op jit(solution)/shard_map/ppermute | solution.py:537
  95.8 22.2 %collective-permute-start.19 = (f32[2,4,17,8,128]{4,3,1,0,2:T(8,128)S(1)}, f32[2,4,17,8,128]{4,3,1,0,2:T(8,128)S(1)}, u32[]{:S(2)}, u32[]{:S(2)}) collective-permute-start(f32[2,4,17,8,128]{4,3,1,0,2:T(8,128)S(1)} %get-tuple-element.88), channel_id=1, source_target_pairs={{0,2},{2,0},{4,6},{6,4},{8,10},{10,8},{12,14},{14,12},{16,18},{18,... | collective-permute-start | bytes 1671176 | tf_op jit(solution)/shard_map/ppermute | solution.py:540
  102.1 4.9 %copy-start.2 = (bf16[16,512,128]{2,1,0:T(8,128)(2,1)S(1)}, bf16[16,512,128]{2,1,0:T(8,128)(2,1)}, u32[]{:S(2)}) copy-start(bf16[16,512,128]{2,1,0:T(8,128)(2,1)} %copy-done.1) | copy-start | bytes 6291460
  117.8 2.0 %collective-permute-start.9 = (f32[2,4,17,8,128]{4,3,2,1,0:T(8,128)S(1)}, f32[2,4,17,8,128]{4,3,2,1,0:T(8,128)S(1)}, u32[]{:S(2)}, u32[]{:S(2)}) collective-permute-start(f32[2,4,17,8,128]{4,3,2,1,0:T(8,128)S(1)} %copy.125), channel_id=1, source_target_pairs={{0,2},{2,0},{4,6},{6,4},{8,10},{10,8},{12,14},{14,12},{16,18},{18,... | collective-permute-start | bytes 1671176 | tf_op jit(solution)/shard_map/ppermute | solution.py:540
  (14 other events, 28.6 us)
